TPU v7x, 32 devices: a whole 2x2x4 slice. The times are simulated.
32 devices in a mesh: rows: 8 (over y, x, core), mem: 4 (over z).
Axes of the slice: x: 2, y: 2, z: 4, core: 2. Of those that a mesh axis runs over, the one named last changes fastest.
Arguments:
- dec_input: bfloat16 [64, 176, 768], P('rows'), may hold values from -6 to 6
- enc_output: bfloat16 [64, 512, 768], P('rows', 'mem'), may hold values from -6 to 6
- dec_segments: int32 [64, 176], P('rows'), may hold values from 0 to 3, as said below
- enc_segments: int32 [64, 512], P('rows'), may hold values from 0 to 3, as said below
- buckets: int32 [176], replicated, may hold values from 0 to 31
- gains: bfloat16 [3, 768], replicated, may hold values from 0.5 to 1.5
- self_query: bfloat16 [768, 768], P(None, 'mem'), may hold values from -0.0546875 to 0.0546875
- self_kv: bfloat16 [2, 768, 768], P(None, None, 'mem'), may hold values from -0.21875 to 0.21875
- self_out: bfloat16 [768, 768], P('mem'), may hold values from -0.625 to 0.625
- rel_table: bfloat16 [32, 12], P(None, 'mem'), may hold values from -4 to 4
- cross_query: bfloat16 [768, 768], P(None, 'mem'), may hold values from -0.0546875 to 0.0546875
- cross_kv: bfloat16 [2, 768, 768], P(None, None, 'mem'), may hold values from -0.21875 to 0.21875
- cross_out: bfloat16 [768, 768], P('mem'), may hold values from -0.875 to 0.875
- ffn_in: bfloat16 [2, 768, 2048], P(None, None, 'mem'), may hold values from -0.21875 to 0.21875
- ffn_out: bfloat16 [2048, 768], P('mem'), may hold values from -0.25 to 0.25
- cotangent: bfloat16 [64, 176, 768], P('rows'), may hold values from -6 to 6
Outputs:
- dec_output: float32 [64, 176, 768], P('rows', 'mem')
- grad_dec_input: float32 [64, 176, 768], P('rows', 'mem')
- grad_enc_output: float32 [64, 512, 768], P('rows', 'mem')
- grad_gains: float32 [3, 768], P(None, 'mem')
- grad_self_query: float32 [768, 768], P(None, 'mem')
- grad_self_kv: float32 [2, 768, 768], P(None, None, 'mem')
- grad_self_out: float32 [768, 768], P('mem')
- grad_rel_table: float32 [32, 12], P(None, 'mem')
- grad_cross_query: float32 [768, 768], P(None, 'mem')
- grad_cross_kv: float32 [2, 768, 768], P(None, None, 'mem')
- grad_cross_out: float32 [768, 768], P('mem')
- grad_ffn_in: float32 [2, 768, 2048], P(None, None, 'mem')
- grad_ffn_out: float32 [2048, 768], P('mem')
Inputs may be any that keep to these rules, and one draw needn't show every extreme that they name: `dec_segments`: each row holds 3 examples with ids 1 to 3 in this order, each one token or longer, followed by one or more padding tokens with id 0. `enc_segments`: each row holds the same 3 example ids as the decoder part of that row, 1 to 3 in this order, each one token or longer, followed by one or more padding tokens with id 0.
All inputs are finite; a program needn't handle non-finite values.
Results may differ from a plain program's by a relative error of at most 0.024.
Values may be sent and summed in bfloat16 or wider, within the bound.
A program may use at most 192 MiB of HBM per device.

v0:
```python
from functools import partial

import jax
import jax.numpy as jnp
from jax import lax
from jax.experimental import pallas as pl
from jax.experimental.pallas import tpu as pltpu
from jax.sharding import PartitionSpec as P

epsilon = 1e-06
negative = -1e30
highest = lax.Precision.HIGHEST
low = jnp.bfloat16
wide = jnp.float32
pair = 128
head_size = 64


def flip(values, bit):
    size = lax.axis_size("rows")
    return lax.ppermute(values, "rows", [(i, i ^ bit) for i in range(size)])


def relative(values, axis, count):
    me = lax.axis_index("mem")
    size = values.shape[axis] // count
    return [
        lax.dynamic_slice_in_dim(values, ((me + step) % count) * size, size, axis)
        for step in range(count)
    ]


block = 8
quarters = 4
MESH = pl.DeviceIdType.MESH


class Place:
    def __init__(self):
        rows = lax.axis_index("rows")
        self.base = (rows // block) * block
        inner = rows - self.base
        self.core = inner % 2
        self.quarter = inner // 2
        self.near = self.quarter % 2
        self.far = self.quarter // 2
        self.me = lax.axis_index("mem")
        self.mem = lax.axis_size("mem")

    def at(self, quarter, core):
        return (self.base + quarter * 2 + core, self.me)

    def other_core(self):
        return self.at(self.quarter, 1 - self.core)

    def other_quarter(self, step):
        return self.at(self.turn(step), self.core)

    def turn(self, step):
        near = (self.near + step % 2) % 2
        far = (self.far + step // 2) % 2
        return far * 2 + near

    def along(self, step):
        rows = self.base + self.quarter * 2 + self.core
        return (rows, (self.me + step) % self.mem)

    def greet(self):
        barrier = pltpu.get_barrier_semaphore()
        count = 0
        for step in range(1, self.mem):
            pl.semaphore_signal(barrier, inc=1, device_id=self.along(step), device_id_type=MESH)
            count += 1
        for quarter in range(quarters):
            for core in range(2):
                if quarter or core:
                    there = self.at(self.turn(quarter), (self.core + core) % 2)
                    pl.semaphore_signal(barrier, inc=1, device_id=there, device_id_type=MESH)
                    count += 1
        pl.semaphore_wait(barrier, count)


def send(source, target, sems, index, there, arrival=None):
    copy = pltpu.make_async_remote_copy(
        src_ref=source,
        dst_ref=target,
        send_sem=sems[0].at[index],
        recv_sem=sems[1].at[index if arrival is None else arrival],
        device_id=there,
        device_id_type=MESH,
    )
    copy.start()
    return copy


def expect(buffer, sems, index, place):
    pltpu.make_async_remote_copy(
        src_ref=buffer,
        dst_ref=buffer,
        send_sem=sems[0].at[index],
        recv_sem=sems[1].at[index],
        device_id=place.other_core(),
        device_id_type=MESH,
    ).wait_recv()


class Chunk:
    def __init__(self, index, own_width, own_hidden):
        self.index = index
        self.is_ffn = index >= 2
        self.part = index % 2
        if self.is_ffn:
            self.k = 3
            self.rows = own_hidden // 16
        else:
            self.k = 1
            self.rows = own_width // 2

    def spot(self, quarter, core):
        if self.is_ffn:
            start = ((quarter * 2 + self.part) * 2 + core) * self.rows
            return pl.ds(0, 3), pl.ds(pl.multiple_of(start, self.rows), self.rows)
        start = core * self.rows
        return (
            pl.ds(self.part * quarters + quarter, 1),
            pl.ds(pl.multiple_of(start, self.rows), self.rows),
        )

    def shard(self, refs, quarter, core):
        k, rows = self.spot(quarter, core)
        return refs[self.is_ffn].at[k, rows]

    def whole(self, refs, steps, quarter, core):
        k, rows = self.spot(quarter, core)
        return refs[self.is_ffn].at[k, steps, rows]


def gather_body(
    attn_ref, ffn_ref, enc_ref, table_ref,
    attn_out, ffn_out, memory_out, tables_out,
    own_enc, local_sems, far_send, far_recv, enc_send, enc_recv, table_send, table_recv,
    flat_send, flat_recv, core_send, core_recv,
):
    place = Place()
    mem = place.mem
    shards = (attn_ref, ffn_ref)
    wholes = (attn_out, ffn_out)
    count = own_enc.shape[0]
    chunks = [Chunk(i, attn_ref.shape[1], ffn_ref.shape[1]) for i in range(4)]
    locals_in = pltpu.make_async_copy(
        enc_ref.at[pl.ds(place.me * count, count)], own_enc, local_sems.at[0]
    )
    locals_in.start()
    locals_out = [
        pltpu.make_async_copy(attn_ref, attn_out.at[:, 0], local_sems.at[1]),
        pltpu.make_async_copy(ffn_ref, ffn_out.at[:, 0], local_sems.at[2]),
    ]
    for copy in locals_out:
        copy.start()
    tables_out[0] = table_ref[...]
    place.greet()
    sent = []

    def start_far(i):
        for step in range(1, mem):
            back = mem - step
            sent.append(
                send(
                    chunks[i].shard(shards, place.quarter, place.core),
                    chunks[i].whole(wholes, back, place.quarter, place.core),
                    (far_send.at[i], far_recv.at[i]), step, place.along(step), back,
                )
            )

    def start_enc():
        for step in range(1, mem):
            back = mem - step
            target = ((place.me + step) % mem) * count
            sent.append(
                send(
                    enc_ref.at[pl.ds(target, count)], memory_out.at[:, back],
                    (enc_send, enc_recv), step, place.along(step), back,
                )
            )

    def pass_on(i, turn):
        piece = chunks[i].whole(wholes, pl.ds(1, mem - 1), place.turn(turn), place.core)
        sent.append(send(piece, piece, (core_send.at[i], core_recv.at[i]), turn, place.other_core()))

    def finish_flat(i):
        for turn in range(1, quarters):
            piece = chunks[i].whole(wholes, pl.ds(1, mem - 1), place.turn(turn), place.core)
            expect(piece, (flat_send.at[i], flat_recv.at[i]), turn, place)
            pass_on(i, turn)

    for step in range(1, mem):
        back = mem - step
        sent.append(
            send(table_ref, tables_out.at[back], (table_send, table_recv), step, place.along(step), back)
        )
    start_far(0)
    start_far(1)
    for i in range(4):
        for step in range(1, mem):
            piece = chunks[i].whole(wholes, step, place.quarter, place.core)
            expect(piece, (far_send.at[i], far_recv.at[i]), step, place)
        if i + 2 < 4:
            start_far(i + 2)
        if i == 2:
            start_enc()
        piece = chunks[i].whole(wholes, pl.ds(1, mem - 1), place.quarter, place.core)
        for turn in range(1, quarters):
            sent.append(
                send(piece, piece, (flat_send.at[i], flat_recv.at[i]), turn, place.other_quarter(turn))
            )
        pass_on(i, 0)
        if i > 0:
            finish_flat(i - 1)
    finish_flat(3)
    locals_in.wait()
    own_out = pltpu.make_async_copy(own_enc, memory_out.at[:, 0], local_sems.at[0])
    own_out.start()
    for i in range(4):
        for turn in range(quarters):
            piece = chunks[i].whole(wholes, pl.ds(1, mem - 1), place.turn(turn), 1 - place.core)
            expect(piece, (core_send.at[i], core_recv.at[i]), turn, place)
    for step in range(1, mem):
        expect(memory_out.at[:, step], (enc_send, enc_recv), step, place)
        expect(tables_out.at[step], (table_send, table_recv), step, place)
    for copy in sent:
        copy.wait_send()
    for copy in locals_out:
        copy.wait()
    own_out.wait()


def gather_all(attn, ffn, enc, table):
    mem = lax.axis_size("mem")
    count = enc.shape[0] // mem
    dma = pltpu.SemaphoreType.DMA
    in_place = pl.BlockSpec(memory_space=pl.ANY)
    held = pl.BlockSpec(memory_space=pltpu.VMEM)
    return pl.pallas_call(
        gather_body,
        in_specs=[held, held, in_place, held],
        out_specs=[in_place, in_place, in_place, held],
        out_shape=[
            jax.ShapeDtypeStruct((attn.shape[0], mem) + attn.shape[1:], low),
            jax.ShapeDtypeStruct((ffn.shape[0], mem) + ffn.shape[1:], low),
            jax.ShapeDtypeStruct((count, mem) + enc.shape[1:], low),
            jax.ShapeDtypeStruct((mem,) + table.shape, low),
        ],
        scratch_shapes=[
            pltpu.VMEM((count,) + enc.shape[1:], low),
            dma((3,)),
            dma((4, mem)), dma((4, mem)),
            dma((mem,)), dma((mem,)),
            dma((mem,)), dma((mem,)),
            dma((4, quarters)), dma((4, quarters)),
            dma((4, quarters)), dma((4, quarters)),
        ],
        compiler_params=pltpu.CompilerParams(collective_id=0, has_side_effects=True),
    )(attn, ffn, enc, table)


def add_planes(total_ref, total_at, more_ref, more_at, k, steps):
    first, size = steps

    def plane(index, carry):
        i, d = index // size, index % size
        added = more_ref[more_at + (i, d)].astype(wide)
        here = total_at + (i, first + d)
        total_ref[here] = (total_ref[here].astype(wide) + added).astype(low)
        return carry

    lax.fori_loop(0, k * size, plane, 0)


def reduce_body(
    attn_ref, ffn_ref, memory_ref, first_ref, second_ref, small_ref,
    attn_out, ffn_out, memory_out, first_out, second_out, small_out,
    held_attn, held_ffn, core_attn, core_ffn, near_attn, near_ffn, last_attn, last_ffn,
    far_attn, far_ffn, small_far, small_flat,
    local_sems, core_send, core_recv, near_send, near_recv, last_send, last_recv,
    far_send, far_recv, flat_send, flat_recv, pass_send, pass_recv,
    move_send, move_recv, small_send, small_recv,
):
    place = Place()
    mem = place.mem
    half = mem // 2
    grads = (attn_ref, ffn_ref)
    outs = (attn_out, ffn_out)
    chunks = [Chunk(i, attn_out.shape[1], ffn_out.shape[1]) for i in range(4)]
    helds = (held_attn, held_ffn)
    cores = (core_attn, core_ffn)
    nears = (near_attn, near_ffn)
    lasts = (last_attn, last_ffn)
    fars = (far_attn, far_ffn)
    near_there = place.other_quarter(1)
    far_there = place.other_quarter(2)
    sent = []
    loads = {}

    def buffers(i):
        kind, part = chunks[i].is_ffn, chunks[i].part
        return tuple(group[kind].at[part] for group in (helds, cores, nears, lasts, fars))

    def load(i):
        held, core = buffers(i)[:2]
        for quarter in range(quarters):
            copy = pltpu.make_async_copy(
                chunks[i].whole(grads, pl.ds(0, mem), quarter, place.core),
                held.at[quarter], local_sems.at[i, quarter],
            )
            copy.start()
            loads[i, quarter] = copy

    def to_core(i):
        core = buffers(i)[1]
        for quarter in range(quarters):
            sent.append(
                send(
                    chunks[i].whole(grads, pl.ds(0, mem), quarter, 1 - place.core),
                    core.at[quarter], (core_send.at[i], core_recv.at[i]), quarter,
                    place.other_core(),
                )
            )

    def from_core(i):
        held, core, near = buffers(i)[:3]
        for quarter in range(quarters):
            loads[i, quarter].wait()
            expect(core.at[quarter], (core_send.at[i], core_recv.at[i]), quarter, place)
            add_planes(held, (quarter,), core, (quarter,), chunks[i].k, (0, mem))
        sems = (near_send.at[i], near_recv.at[i])
        for bit in range(2):
            quarter = bit * 2 + (1 - place.near)
            sent.append(
                send(
                    held.at[quarter, :, pl.ds(0, half)], near.at[0, bit], sems, bit, near_there
                )
            )
            quarter = (1 - place.far) * 2 + bit
            sent.append(
                send(
                    held.at[quarter, :, pl.ds(half, half)], near.at[1, bit], sems, 2 + bit, far_there
                )
            )

    def from_near(i):
        held, core, near, last = buffers(i)[:4]
        sems = (near_send.at[i], near_recv.at[i])
        for bit in range(2):
            expect(near.at[0, bit], sems, bit, place)
            add_planes(
                held, (bit * 2 + place.near,), near, (0, bit), chunks[i].k, (0, half)
            )
            expect(near.at[1, bit], sems, 2 + bit, place)
            add_planes(
                held, (place.far * 2 + bit,), near, (1, bit), chunks[i].k, (half, half)
            )
        sems = (last_send.at[i], last_recv.at[i])
        quarter = (1 - place.far) * 2 + place.near
        sent.append(send(held.at[quarter, :, pl.ds(0, half)], last.at[0], sems, 0, far_there))
        quarter = place.far * 2 + (1 - place.near)
        sent.append(send(held.at[quarter, :, pl.ds(half, half)], last.at[1], sems, 1, near_there))

    def from_last(i):
        held, _, _, last, far = buffers(i)
        sems = (last_send.at[i], last_recv.at[i])
        for part in range(2):
            expect(last.at[part], sems, part, place)
            add_planes(
                held, (place.quarter,), last, (part,), chunks[i].k, (part * half, half)
            )
        for step in range(1, mem):
            back = mem - step
            sent.append(
                send(
                    held.at[place.quarter, :, step], far.at[back],
                    (far_send.at[i], far_recv.at[i]), step, place.along(step), back,
                )
            )

    def from_far(i):
        held, _, _, _, far = buffers(i)
        for step in range(1, mem):
            expect(far.at[step], (far_send.at[i], far_recv.at[i]), step, place)
        kind = chunks[i].is_ffn
        k_at, rows_at = chunks[i].spot(place.quarter, place.core)
        for k in range(chunks[i].k):
            total = held[place.quarter, k, 0].astype(wide)
            for step in range(1, mem):
                total = total + far[step, k].astype(wide)
            outs[kind][k_at.start + k, rows_at, :] = total.astype(low)
        piece = chunks[i].shard(outs, place.quarter, place.core)
        for turn in range(1, quarters):
            sent.append(
                send(piece, piece, (flat_send.at[i], flat_recv.at[i]), turn, place.other_quarter(turn))
            )
        sent.append(send(piece, piece, (pass_send.at[i], pass_recv.at[i]), 0, place.other_core()))

    def from_flat(i):
        for turn in range(1, quarters):
            piece = chunks[i].shard(outs, place.turn(turn), place.core)
            expect(piece, (flat_send.at[i], flat_recv.at[i]), turn, place)
            sent.append(
                send(piece, piece, (pass_send.at[i], pass_recv.at[i]), turn, place.other_core())
            )

    def from_pass(i):
        for turn in range(quarters):
            piece = chunks[i].shard(outs, place.turn(turn), 1 - place.core)
            expect(piece, (pass_send.at[i], pass_recv.at[i]), turn, place)

    moves = (
        (lambda step: memory_ref.at[:, step], memory_out),
        (lambda step: first_ref.at[step], first_out),
        (lambda step: second_ref.at[step], second_out),
    )
    for i in range(4):
        load(i)
    stays = []
    for index, (source, target) in enumerate(moves):
        copy = pltpu.make_async_copy(source(0), target.at[place.me], local_sems.at[4, index])
        copy.start()
        stays.append(copy)
    place.greet()
    order = (2, 3, 1, 0)
    for i in order:
        to_core(i)
    for index, (source, target) in enumerate(moves):
        for step in range(1, mem):
            sent.append(
                send(
                    source(step), target.at[place.me], (move_send.at[index], move_recv.at[index]),
                    step, place.along(step), mem - step,
                )
            )
    for step in range(1, mem):
        back = mem - step
        sent.append(
            send(small_ref.at[step], small_far.at[back], (small_send, small_recv), step, place.along(step), back)
        )
    phases = (from_core, from_near, from_last, from_far, from_flat, from_pass)
    for time in range(len(order) + len(phases) - 1):
        for slot, i in enumerate(order):
            if 0 <= time - slot < len(phases):
                phases[time - slot](i)
        if time == 1:
            small = small_ref[0]
            for step in range(1, mem):
                expect(small_far.at[step], (small_send, small_recv), step, place)
                small = small + small_far[step]
            small_flat[0] = small
            for turn in range(1, block):
                there = place.at(place.turn(turn // 2), (place.core + turn % 2) % 2)
                sent.append(
                    send(small_flat.at[0], small_flat.at[turn], (small_send, small_recv), mem + turn, there)
                )
    small = small_flat[0]
    for turn in range(1, block):
        expect(small_flat.at[turn], (small_send, small_recv), mem + turn, place)
        small = small + small_flat[turn]
    small_out[...] = small
    for index, (source, target) in enumerate(moves):
        for step in range(1, mem):
            expect(
                target.at[(place.me + step) % mem],
                (move_send.at[index], move_recv.at[index]), step, place,
            )
    for copy in sent:
        copy.wait_send()
    for copy in stays:
        copy.wait()


def reduce_all(attn, ffn, memory, first, second, small):
    mem = lax.axis_size("mem")
    model = attn.shape[-1]
    dma = pltpu.SemaphoreType.DMA
    in_place = pl.BlockSpec(memory_space=pl.ANY)
    held = pl.BlockSpec(memory_space=pltpu.VMEM)
    chunks = [Chunk(i, attn.shape[2], ffn.shape[2]) for i in (0, 2)]

    def both(*shape_of):
        return [
            pltpu.VMEM((2,) + tuple(s(c) if callable(s) else s for s in shape_of), low)
            for c in chunks
        ]

    def k(chunk):
        return chunk.k

    def rows(chunk):
        return chunk.rows

    sem_shapes = ((4, quarters), (4, quarters), (4, 2), (4, mem), (4, quarters), (4, quarters), (3, mem), (mem + block,))
    sems = [dma((5, quarters))]
    for shape in sem_shapes:
        sems += [dma(shape), dma(shape)]
    return pl.pallas_call(
        reduce_body,
        in_specs=[in_place, in_place, held, held, held, held],
        out_specs=[held, held, in_place, in_place, in_place, held],
        out_shape=[
            jax.ShapeDtypeStruct((attn.shape[0],) + attn.shape[2:], low),
            jax.ShapeDtypeStruct((ffn.shape[0],) + ffn.shape[2:], low),
            jax.ShapeDtypeStruct((mem, memory.shape[0]) + memory.shape[2:], low),
            jax.ShapeDtypeStruct(first.shape, low),
            jax.ShapeDtypeStruct(second.shape, low),
            jax.ShapeDtypeStruct(small.shape[1:], wide),
        ],
        scratch_shapes=both(quarters, k, mem, rows, model)
        + both(quarters, k, mem, rows, model)
        + both(2, 2, k, mem // 2, rows, model)
        + both(2, k, mem // 2, rows, model)
        + both(mem, k, rows, model)
        + [pltpu.VMEM((mem,) + small.shape[1:], wide), pltpu.VMEM((block,) + small.shape[1:], wide)]
        + sems,
        compiler_params=pltpu.CompilerParams(collective_id=1, has_side_effects=True),
    )(attn, ffn, memory, first, second, small)


def sum_blocks(values):
    bit = block
    while bit < lax.axis_size("rows"):
        values = values + flip(values, bit)
        bit *= 2
    return values


def dot(left, right, left_dim, right_dim):
    return lax.dot_general(
        left, right, (((left_dim,), (right_dim,)), ((), ())), preferred_element_type=wide
    )


def lanes_of(half):
    lane = lax.broadcasted_iota(jnp.int32, (1, pair), 1)
    return ((lane // head_size) == half).astype(wide)


def skewed(row, height):
    spread = jnp.broadcast_to(row, (height, row.shape[1]))
    return pltpu.roll(spread, 0, 1, stride=1, stride_axis=0)


def attend_body(causal, q_ref, k_ref, v_ref, dec_ref, key_ref, *rest):
    if causal:
        bias_ref, out_ref, weight_ref = rest
    else:
        out_ref, weight_ref = rest
    queries, keys_in, values_in = q_ref[0], k_ref[0], v_ref[0]
    rows, keys = queries.shape[0], keys_in.shape[0]
    allowed = dec_ref[0] == key_ref[0]
    if causal:
        i = lax.broadcasted_iota(jnp.int32, (rows, keys), 0)
        j = lax.broadcasted_iota(jnp.int32, (rows, keys), 1)
        allowed = allowed & (i >= j)
    mixed = jnp.zeros((rows, pair), wide)
    for half in range(2):
        lanes = lanes_of(half)
        scores = dot(queries * lanes.astype(low), keys_in, 1, 1)
        if causal:
            scores = scores + skewed(bias_ref[0, half : half + 1, :], rows)[:, :keys]
        scores = jnp.where(allowed, scores, negative)
        raised = jnp.exp(scores - jnp.max(scores, axis=-1, keepdims=True))
        scale = 1.0 / jnp.sum(raised, axis=-1, keepdims=True)
        weights = (raised * scale).astype(low)
        weight_ref[0, half] = weights
        mixed = mixed + dot(weights, values_in, 1, 0) * lanes
    out_ref[0] = mixed.astype(low)


def attend_back_body(causal, w_ref, q_ref, k_ref, v_ref, g_ref, *rest):
    if causal:
        out_ref, dist_ref = rest
    else:
        dq_ref, dkv_ref = rest
    queries, keys_in, values_in, grad = q_ref[0], k_ref[0], v_ref[0], g_ref[0]
    rows, keys = queries.shape[0], keys_in.shape[0]
    dq = jnp.zeros((rows, pair), wide)
    dk = jnp.zeros((keys, pair), wide)
    dv = jnp.zeros((keys, pair), wide)
    for half in range(2):
        lanes = lanes_of(half)
        weights = w_ref[0, half]
        weights_wide = weights.astype(wide)
        grad_weights = dot(grad * lanes.astype(low), values_in, 1, 1)
        inner = jnp.sum(grad_weights * weights_wide, axis=-1, keepdims=True)
        grad_scores = (weights_wide * (grad_weights - inner)).astype(low)
        dv = dv + dot(weights, grad, 0, 0) * lanes
        dq = dq + dot(grad_scores, keys_in, 1, 0) * lanes
        dk = dk + dot(grad_scores, queries, 0, 0) * lanes
        if causal:
            width = dist_ref.shape[-1]
            i = lax.broadcasted_iota(jnp.int32, (rows, rows), 0)
            j = lax.broadcasted_iota(jnp.int32, (rows, rows), 1)
            upside_down = dot((i + j == rows - 1).astype(wide).astype(low), grad_scores, 1, 0)
            padded = jnp.concatenate(
                [upside_down, jnp.zeros((rows, width - keys), wide)], axis=1
            )
            turned = pltpu.roll(padded, 0, 1, stride=1, stride_axis=0)
            dist_ref[0, 0, half : half + 1, :] = jnp.sum(turned, axis=0, keepdims=True)
    if causal:
        out_ref[0, 0] = dq.astype(low)
        out_ref[0, 1] = dk.astype(low)
        out_ref[0, 2] = dv.astype(low)
    else:
        dq_ref[0] = dq.astype(low)
        dkv_ref[0, 0] = dk.astype(low)
        dkv_ref[0, 1] = dv.astype(low)


def column(length, offset):
    return pl.BlockSpec((1, length, pair), lambda r, p: (r, 0, p + offset))


def cost_of(count, rows, keys, pairs, dots):
    return pl.CostEstimate(
        flops=count * pairs * 2 * dots * 2 * rows * keys * pair,
        bytes_accessed=count * pairs * (2 * rows * keys * 2 + 4 * keys * pair * 2),
        transcendentals=count * pairs * 2 * rows * keys,
    )


def whole_row(*shape):
    return pl.BlockSpec((1,) + shape, lambda r, p: (r,) + (0,) * len(shape))


def attend(queries, sides, offsets, dec_ids, key_ids, bias):
    count, rows, _ = queries.shape
    keys = sides.shape[1]
    pairs = queries.shape[2] // pair if bias is None else bias.shape[0]
    width = pairs * pair
    in_specs = [
        column(rows, 0),
        column(keys, offsets[0]),
        column(keys, offsets[1]),
        whole_row(rows, 1),
        whole_row(1, keys),
    ]
    operands = [queries, sides, sides, dec_ids[:, :, None], key_ids[:, None, :]]
    if bias is not None:
        in_specs.append(pl.BlockSpec((1, 2, bias.shape[2]), lambda r, p: (p, 0, 0)))
        operands.append(bias)
    return pl.pallas_call(
        partial(attend_body, bias is not None),
        grid=(count, pairs),
        in_specs=in_specs,
        out_specs=[
            column(rows, 0),
            pl.BlockSpec((1, 2, rows, keys), lambda r, p: (r, p, 0, 0)),
        ],
        out_shape=[
            jax.ShapeDtypeStruct((count, rows, width), low),
            jax.ShapeDtypeStruct((count, pairs * 2, rows, keys), low),
        ],
        cost_estimate=cost_of(count, rows, keys, pairs, 2),
    )(*operands)


def attend_back(weights, queries, sides, offsets, grad, dist_width):
    count, heads, rows, keys = weights.shape
    pairs = heads // 2
    width = pairs * pair
    causal = dist_width is not None
    if causal:
        out_specs = [
            pl.BlockSpec((1, 3, rows, pair), lambda r, p: (r, 0, 0, p)),
            pl.BlockSpec((1, 1, 2, dist_width), lambda r, p: (r, p, 0, 0)),
        ]
        out_shape = [
            jax.ShapeDtypeStruct((count, 3, rows, width), low),
            jax.ShapeDtypeStruct((count, pairs, 2, dist_width), wide),
        ]
    else:
        out_specs = [
            column(rows, 0),
            pl.BlockSpec((1, 2, keys, pair), lambda r, p: (r, 0, 0, p)),
        ]
        out_shape = [
            jax.ShapeDtypeStruct((count, rows, width), low),
            jax.ShapeDtypeStruct((count, 2, keys, width), low),
        ]
    return pl.pallas_call(
        partial(attend_back_body, causal),
        grid=(count, pairs),
        in_specs=[
            pl.BlockSpec((1, 2, rows, keys), lambda r, p: (r, p, 0, 0)),
            column(rows, 0),
            column(keys, offsets[0]),
            column(keys, offsets[1]),
            column(rows, 0),
        ],
        out_specs=out_specs,
        out_shape=out_shape,
        cost_estimate=cost_of(count, rows, keys, pairs, 4),
    )(weights, queries, sides, sides, grad)


def rms(values, gain):
    scale = lax.rsqrt(jnp.mean(values * values, axis=-1, keepdims=True) + epsilon)
    return (values * scale * gain).astype(low), scale


def rms_back(values, scale, gain, grad):
    grad_gain = jnp.sum(grad * values * scale, axis=(0, 1))
    scaled = grad * gain
    inner = jnp.mean(scaled * values, axis=-1, keepdims=True)
    return scaled * scale - values * (scale * scale * scale * inner), grad_gain


def times_t(values, weight):
    return jnp.einsum("rtd,cd->rtc", values, weight, preferred_element_type=wide)


def times(values, weight):
    return jnp.einsum("rtc,cd->rtd", values, weight, preferred_element_type=wide)


def weight_grad(grads, values):
    return jnp.einsum("rtc,rtd->cd", grads, values, preferred_element_type=wide).astype(low)


def gated(gate, upward):
    return jax.nn.gelu(gate, approximate=True) * upward


def shards(
    dec_input,
    enc_output,
    dec_segments,
    enc_segments,
    buckets,
    gains,
    self_query,
    self_kv,
    self_out,
    rel_table,
    cross_query,
    cross_kv,
    cross_out,
    ffn_in,
    ffn_out,
    cotangent,
):
    mem = lax.axis_size("mem")
    me = lax.axis_index("mem")
    group, dec_len, model = dec_input.shape
    count = group // mem
    own_heads = rel_table.shape[1]
    own_width = self_query.shape[1]
    width = own_width * mem
    pairs = width // pair
    own_hidden = ffn_out.shape[0]
    gain_values = gains.astype(wide)
    bucket_count = rel_table.shape[0]

    attn_shard = jnp.stack(
        [self_query.T, self_kv[0].T, self_kv[1].T, self_out]
        + [cross_query.T, cross_kv[0].T, cross_kv[1].T, cross_out]
    )
    ffn_shard = jnp.stack([ffn_in[0].T, ffn_in[1].T, ffn_out])
    padded_table = jnp.pad(rel_table, ((0, 0), (0, pair - own_heads)))
    attn_weights, ffn_weights, memory, tables = gather_all(
        attn_shard, ffn_shard, enc_output, padded_table
    )
    attn_weights = attn_weights.reshape(-1, width, model)
    ffn_weights = ffn_weights.reshape(-1, model)
    memory = memory.reshape(count, -1, model)

    def mine(values):
        return lax.dynamic_slice_in_dim(values, me * count, count, 0)

    inputs = mine(dec_input).astype(wide)
    grad_out = mine(cotangent)
    dec_ids = mine(dec_segments)
    enc_ids = jnp.concatenate(relative(mine(enc_segments), 1, mem), axis=1)
    enc_len = memory.shape[1]

    lane_count = -(-dec_len // pair) * pair
    turned = jnp.concatenate(
        [
            buckets[:1],
            jnp.full((lane_count - dec_len,), -1, buckets.dtype),
            jnp.flip(buckets[1:]),
        ]
    )
    def one_hot_of(ids):
        return (ids[:, None] == jnp.arange(bucket_count)[None, :]).astype(wide)

    one_hot = one_hot_of(turned)
    table = tables[:, :, :own_heads].astype(wide)
    bias = jnp.einsum("mbh,lb->mhl", table, one_hot, precision=highest)
    bias = bias.reshape(pairs, 2, lane_count)

    qkv_weight = attn_weights[:3].reshape(3 * width, model)
    self_out_weight = attn_weights[3]
    cross_query_weight = attn_weights[4]
    cross_kv_weight = attn_weights[5:7].reshape(2 * width, model)
    cross_out_weight = attn_weights[7]
    normed_one, scale_one = rms(inputs, gain_values[0])
    qkv = times_t(normed_one, qkv_weight).astype(low)
    self_mixed, self_weights = attend(
        qkv, qkv, (pairs, 2 * pairs), dec_ids, dec_ids, bias
    )
    first = inputs + times(self_mixed, self_out_weight)
    normed_two, scale_two = rms(first, gain_values[1])
    cross_kv_values = times_t(memory, cross_kv_weight).astype(low)
    cross_queries = times_t(normed_two, cross_query_weight).astype(low)
    cross_mixed, cross_weights = attend(
        cross_queries, cross_kv_values, (0, pairs), dec_ids, enc_ids, None
    )
    second = first + times(cross_mixed, cross_out_weight)
    normed_three, scale_three = rms(second, gain_values[2])

    hidden_width = mem * own_hidden
    in_weight = ffn_weights[: 2 * hidden_width]
    out_weight = ffn_weights[2 * hidden_width :]
    gate_up = times_t(normed_three, in_weight)
    hidden_float, pull = jax.vjp(gated, gate_up[..., :hidden_width], gate_up[..., hidden_width:])
    hidden = hidden_float.astype(low)
    output = second + times(hidden, out_weight)
    grad_gate, grad_up = pull(times_t(grad_out, out_weight))
    grad_gate_up = jnp.concatenate([grad_gate.astype(low), grad_up.astype(low)], axis=-1)
    grad_three = times(grad_gate_up, in_weight)
    ffn_grads = jnp.concatenate(
        [weight_grad(grad_gate_up, normed_three), weight_grad(hidden, grad_out)]
    ).reshape(3, mem, own_hidden, model)

    grad_wide = grad_out.astype(wide)
    back, gain_three = rms_back(second, scale_three, gain_values[2], grad_three)
    grad_second = grad_wide + back
    grad_second_low = grad_second.astype(low)
    grad_cross_mixed = times_t(grad_second_low, cross_out_weight).astype(low)
    grad_cross_out = weight_grad(cross_mixed, grad_second_low)
    cross_dq, cross_dkv = attend_back(
        cross_weights, cross_queries, cross_kv_values, (0, pairs), grad_cross_mixed, None
    )
    grad_cross_query = weight_grad(cross_dq, normed_two)
    grad_cross_kv = jnp.einsum(
        "rmsc,rsd->mcd", cross_dkv, memory, preferred_element_type=wide
    ).astype(low)
    grad_memory = jnp.einsum(
        "rmsc,mcd->rsd",
        cross_dkv,
        cross_kv_weight.reshape(2, width, model),
        preferred_element_type=wide,
    ).astype(low)
    back, gain_two = rms_back(
        first, scale_two, gain_values[1], times(cross_dq, cross_query_weight)
    )
    grad_first = grad_second + back
    grad_first_low = grad_first.astype(low)
    grad_self_mixed = times_t(grad_first_low, self_out_weight).astype(low)
    grad_self_out = weight_grad(self_mixed, grad_first_low)
    self_grads, distance_sums = attend_back(
        self_weights, qkv, qkv, (pairs, 2 * pairs), grad_self_mixed, lane_count
    )
    grad_qkv = jnp.einsum(
        "rmtc,rtd->mcd", self_grads, normed_one, preferred_element_type=wide
    ).astype(low)
    attn_grads = jnp.concatenate(
        [
            grad_qkv.reshape(3 * width, model),
            grad_self_out,
            grad_cross_query,
            grad_cross_kv.reshape(2 * width, model),
            grad_cross_out,
        ]
    ).reshape(8, mem, own_width, model)
    grad_one = jnp.einsum(
        "rmtc,mcd->rtd",
        self_grads,
        qkv_weight.reshape(3, width, model),
        preferred_element_type=wide,
    )
    back, gain_one = rms_back(inputs, scale_one, gain_values[0], grad_one)
    grad_input = grad_first + back

    falling = jnp.concatenate(
        [jnp.flip(buckets), jnp.full((lane_count - dec_len,), -1, buckets.dtype)]
    )
    grad_table = jnp.einsum(
        "lb,hl->hb",
        one_hot_of(falling),
        jnp.sum(distance_sums, axis=0).reshape(2 * pairs, lane_count),
        precision=highest,
    )
    gain_grads = jnp.concatenate(
        relative(jnp.stack([gain_one, gain_two, gain_three]), 1, mem), axis=0
    ).reshape(mem, 3 * own_width)
    small = jnp.concatenate(
        [gain_grads, grad_table.reshape(mem, own_heads * bucket_count)], axis=1
    )
    small_size = small.shape[1]
    small = jnp.pad(small, ((0, 0), (0, 8 * pair - small_size))).reshape(mem, 8, pair)
    attn_sums, ffn_sums, grad_memory, output, grad_input, small = reduce_all(
        attn_grads,
        ffn_grads,
        grad_memory.reshape(count, mem, enc_len // mem, model),
        jnp.stack(relative(output.astype(low), 1, mem)),
        jnp.stack(relative(grad_input.astype(low), 1, mem)),
        small,
    )
    attn_sums = sum_blocks(attn_sums).astype(wide)
    ffn_sums = sum_blocks(ffn_sums).astype(wide)
    small = sum_blocks(small).reshape(-1)
    split = 3 * own_width

    def columns(values):
        return jnp.swapaxes(values, -1, -2)

    return (
        output.reshape(group, -1, model).astype(wide),
        grad_input.reshape(group, -1, model).astype(wide),
        grad_memory.reshape(group, -1, model).astype(wide),
        small[:split].reshape(3, own_width),
        columns(attn_sums[0]),
        columns(attn_sums[1:3]),
        attn_sums[3],
        small[split:small_size].reshape(own_heads, bucket_count).T,
        columns(attn_sums[4]),
        columns(attn_sums[5:7]),
        attn_sums[7],
        columns(ffn_sums[:2]),
        ffn_sums[2],
    )


def solution(mesh):
    in_specs = (
        P("rows", None, None),
        P("rows", "mem", None),
        P("rows", None),
        P("rows", None),
        P(),
        P(),
        P(None, "mem"),
        P(None, None, "mem"),
        P("mem", None),
        P(None, "mem"),
        P(None, "mem"),
        P(None, None, "mem"),
        P("mem", None),
        P(None, None, "mem"),
        P("mem", None),
        P("rows", None, None),
    )
    out_specs = (
        P("rows", "mem", None),
        P("rows", "mem", None),
        P("rows", "mem", None),
        P(None, "mem"),
        P(None, "mem"),
        P(None, None, "mem"),
        P("mem", None),
        P(None, "mem"),
        P(None, "mem"),
        P(None, None, "mem"),
        P("mem", None),
        P(None, None, "mem"),
        P("mem", None),
    )
    return jax.shard_map(shards, mesh=mesh, in_specs=in_specs, out_specs=out_specs, check_vma=False)
```

profile of v0, /device:TPU:25, one launch (start us, length us, event | category | flops | bytes accessed | tf_op | source)
XLA Modules:
  0.0 454.4 jit_solution(8635299432015262902)
XLA Ops:
  13.3 1.7 pad_maximum_fusion.2.ffn_ref
  17.8 101.7 %shard_map.255 = (bf16[8,4,192,768]{3,2,1,0:T(8,128)(2,1)}, bf16[3,4,512,768]{3,2,1,0:T(8,128)(2,1)}, bf16[2,4,128,768]{3,2,1,0:T(8,128)(2,1)}, bf16[4,32,128]{2,1,0:T(8,128)(2,1)}) custom-call(bf16[8,192,768]{2,1,0:T(8,128)(2,1)} %copy-done.11, bf16[3,512,768]{2,1,0:T(8,128)(2,1)} %pad_maximum_fusion.2.ffn_ref, bf16[8,128,768]{2,1,0:T(8,128)(2,1)} %enc_ref.1, ...), custom_call_target="tpu_custom_call" | custom-call | tf_op jit(solution)/shard_map/pallas_call | solution.py:243
  121.1 2.0 slice.130
  123.1 7.2 %convolution_convert_fusion.1.k_ref.v_ref = bf16[2,512,1536]{2,1,0:T(8,128)(2,1)} fusion(bf16[2,512,768]{2,1,0:T(8,128)(2,1)} %bitcast.234, bf16[1536,768,1]{1,0,2:T(8,128)(2,1)S(1)} %bitcast.225), kind=kOutput, calls=%fused_computation.8 | convolution fusion | flops 2417491968 | bytes 7077888 | tf_op jit(solution)/shard_map/rtd,cd->rtc/dot_general | solution.py:716
  130.3 1.9 slice.125
  132.2 3.1 slice.133
  137.7 3.8 convolution_convert_fusion.q_ref.k_ref.v_ref
  141.5 13.0 %shard_map.256 = (bf16[2,176,768]{2,1,0:T(8,128)(2,1)}, bf16[2,12,176,176]{3,2,1,0:T(8,128)(2,1)}) custom-call(bf16[2,176,2304]{2,1,0:T(8,128)(2,1)} %convolution_convert_fusion.q_ref.k_ref.v_ref, bf16[2,176,2304]{2,1,0:T(8,128)(2,1)} %convolution_convert_fusion.q_ref.k_ref.v_ref, bf16[2,176,2304]{2,1,0:T(8,128)(2,1)} %convolution_convert_fusion.q_ref.k_ref.v_ref, ...), custom_call_target="tpu_custom_call" | custom-call | flops 380633088 | bytes 3649536 | tf_op jit(solution)/shard_map/pallas_call | solution.py:648
  154.5 1.9 multiply_reduce_fusion.5
  157.9 13.4 %shard_map.257 = (bf16[2,176,768]{2,1,0:T(8,128)(2,1)}, bf16[2,12,176,512]{3,2,1,0:T(8,128)(2,1)}) custom-call(bf16[2,176,768]{2,1,0:T(8,128)(2,1)} %convolution_convert_fusion.4.q_ref, bf16[2,512,1536]{2,1,0:T(8,128)(2,1)} %convolution_convert_fusion.1.k_ref.v_ref, bf16[2,512,1536]{2,1,0:T(8,128)(2,1)} %convolution_convert_fusion.1.k_ref.v_ref, ...), custom_call_target="tpu_custom_call" | custom-call | flops 1107296256 | bytes 10616832 | tf_op jit(solution)/shard_map/pallas_call | solution.py:648
  171.3 2.1 multiply_reduce_fusion.4
  173.5 5.6 %fusion.33 = f32[2,176,4096]{2,1,0:T(8,128)S(1)} fusion(bf16[4096,768,1]{1,0,2:T(8,128)(2,1)} %bitcast.214, f32[2,176,768]{2,1,0:T(8,128)S(1)} %get-tuple-element.117, f32[768]{0:T(1024)S(1)} %get-tuple-element.81, f32[2,176]{1,0:T(2,128)S(1)} %add_rsqrt_fusion), kind=kOutput, calls=%fused_computation.100 | convolution fusion | flops 2215403520 | bytes 13144448 | tf_op jit(solution)/shard_map/rtd,cd->rtc/dot_general | solution.py:716
  179.2 3.6 fusion.6
  182.8 2.3 fusion.11
  185.2 2.6 multiply_reduce_fusion
  190.6 14.7 %shard_map.258 = (bf16[2,176,768]{2,1,0:T(8,128)(2,1)}, bf16[2,2,512,768]{3,2,1,0:T(8,128)(2,1)}) custom-call(bf16[2,12,176,512]{3,2,1,0:T(8,128)(2,1)} %get-tuple-element.38.w_ref, bf16[2,176,768]{2,1,0:T(8,128)(2,1)} %convolution_convert_fusion.4.q_ref, bf16[2,512,1536]{2,1,0:T(8,128)(2,1)} %convolution_convert_fusion.1.k_ref.v_ref, ...), custom_call_target="tpu_custom_call" | custom-call | flops 2214592512 | bytes 10616832 | tf_op jit(solution)/shard_map/pallas_call | solution.py:687
  205.2 6.4 %bitcast_convert_fusion.4 = bf16[2,512,768]{2,1,0:T(8,128)(2,1)} fusion(bf16[2,2,512,768]{3,2,1,0:T(8,128)(2,1)} %get-tuple-element.41, bf16[2,768,768,1]{2,1,0,3:T(8,128)(2,1)} %bitcast.226), kind=kOutput, calls=%fused_computation.10 | convolution fusion | flops 2416705536 | bytes 7077888 | tf_op jit(solution)/shard_map/rmsc,mcd->rsd/dot_general | solution.py:846
  214.6 13.7 %shard_map.259 = (bf16[2,3,176,768]{3,2,1,0:T(8,128)(2,1)}, f32[2,6,2,256]{3,2,1,0:T(2,128)}) custom-call(bf16[2,12,176,176]{3,2,1,0:T(8,128)(2,1)} %get-tuple-element.33.w_ref, bf16[2,176,2304]{2,1,0:T(8,128)(2,1)} %convolution_convert_fusion.q_ref.k_ref.v_ref, bf16[2,176,2304]{2,1,0:T(8,128)(2,1)} %convolution_convert_fusion.q_ref.k_ref.v_ref, ...), custom_call_target="tpu_custom_call" | custom-call | flops 761266176 | bytes 3649536 | tf_op jit(solution)/shard_map/pallas_call | solution.py:687
  228.3 5.1 %fusion.20 = (f32[768]{0:T(1024)S(1)}, f32[2,176]{1,0:T(2,128)S(1)}, f32[2,176,768]{2,1,0:T(8,128)}) fusion(f32[2,176]{1,0:T(2,128)S(1)} %add_rsqrt_fusion.2, bf16[8,176,768]{2,1,0:T(8,128)(2,1)} %param.16, s32[]{:T(128)S(6)} %select_n.99, f32[768]{0:T(1024)S(1)} %get-tuple-element.83, bf16[2,3,176,768]{3,2,1,0:T(8,128)(2,1)} %get-tuple-element.40, ...), kind=kOutput, calls=%fused_computation.55 | convolution fusion | flops 1247599488 | bytes 6791940 | tf_op jit(solution)/shard_map/rmtc,mcd->rtd/dot_general | solution.py:874
  233.5 1.7 fusion.18
  239.4 3.1 bitcast_convert_fusion.3
  242.5 3.0 bitcast_convert_fusion.2
  245.6 3.3 bitcast_convert_fusion.1
  249.0 4.2 bitcast_convert_fusion
  253.2 15.8 %pad_maximum_fusion = bf16[6144,768]{1,0:T(8,128)(2,1)} fusion(bf16[2048,768]{1,0:T(8,128)(2,1)S(1)} %bitcast_convert_fusion.2, bf16[4096,768]{1,0:T(8,128)(2,1)S(1)} %bitcast_convert_fusion), kind=kLoop, calls=%fused_computation.1 | loop fusion | flops 18874368 | bytes 18874368 | tf_op jit(solution)/shard_map/concatenate | solution.py:829
  269.0 2.1 constant_dynamic-update-slice_fusion.1
  271.1 1.8 fusion.8
  273.0 1.9 fusion.9
  277.0 1.8 fusion.10
  278.9 157.0 %shard_map.260 = (bf16[8,192,768]{2,1,0:T(8,128)(2,1)}, bf16[3,512,768]{2,1,0:T(8,128)(2,1)}, bf16[4,2,128,768]{3,2,1,0:T(8,128)(2,1)}, bf16[4,2,44,768]{3,2,1,0...) custom-call(bf16[8,4,192,768]{3,2,1,0:T(8,128)(2,1)} %bitcast.55.attn_ref, ...), custom_call_target="tpu_custom_call" | custom-call | tf_op jit(solution)/shard_map/pallas_call | solution.py:502
  443.1 2.0 bitcast_convert_fusion.8
  451.8 2.4 copy.50
  (170 shorter events, 46.6 us)
Async XLA Ops:
  0.6 6.5 %copy-start = (s32[8,176]{1,0:T(8,128)S(1)}, s32[8,176]{1,0:T(8,128)}, u32[]{:S(2)}) copy-start(s32[8,176]{1,0:T(8,128)} %param.18) | copy-start | bytes 16900
  121.1 9.2 %copy-start.6 = (bf16[3,4,512,768]{3,2,1,0:T(8,128)(2,1)S(1)}, bf16[3,4,512,768]{3,2,1,0:T(8,128)(2,1)}, u32[]{:S(2)}) copy-start(bf16[3,4,512,768]{3,2,1,0:T(8,128)(2,1)} %get-tuple-element.34) | copy-start | bytes 28311556
  123.1 7.2 %copy-start.14 = (bf16[2,4,192,768]{3,2,1,0:T(8,128)(2,1)}, bf16[2,4,192,768]{3,2,1,0:T(8,128)(2,1)S(1)}, u32[]{:S(2)}) copy-start(bf16[2,4,192,768]{3,2,1,0:T(8,128)(2,1)S(1)} %slice.130) | copy-start | bytes 7077892
  123.1 12.2 %slice-start = ((s8[9437184]{0:T(1024)(128)(4,1)}), s8[4194304]{0:T(1024)(128)(4,1)S(1)}, s32[]{:S(2)}) async-start(s8[9437184]{0:T(1024)(128)(4,1)} %bitcast.212), calls=%async_computation | async-start | bytes 8388608
  123.1 12.2 %slice-start.1 = ((s8[9437184]{0:T(1024)(128)(4,1)}), s8[4194304]{0:T(1024)(128)(4,1)S(1)}, s32[]{:S(2)}) async-start(s8[9437184]{0:T(1024)(128)(4,1)} %bitcast.212), calls=%async_computation.1 | async-start | bytes 8388608
  132.2 3.1 slice-start.2
  135.5 2.1 copy-start.9
  173.4 14.4 %copy-start.7 = (f32[2,176,768]{2,1,0:T(8,128)}, f32[2,176,768]{2,1,0:T(8,128)S(1)}, u32[]{:S(2)}) copy-start(f32[2,176,768]{2,1,0:T(8,128)S(1)} %get-tuple-element.117) | copy-start | bytes 3244036
  173.5 5.7 %copy-start.10 = (bf16[1,4,512,768]{3,2,1,0:T(8,128)(2,1)S(1)}, bf16[1,4,512,768]{3,2,1,0:T(8,128)(2,1)}, u32[]{:S(2)}) copy-start(bf16[1,4,512,768]{3,2,1,0:T(8,128)(2,1)} %slice.125) | copy-start | bytes 9437188
  173.5 5.7 %copy-start.29 = (bf16[8,176,768]{2,1,0:T(8,128)(2,1)S(1)}, bf16[8,176,768]{2,1,0:T(8,128)(2,1)}, u32[]{:S(2)}) copy-start(bf16[8,176,768]{2,1,0:T(8,128)(2,1)} %param.31) | copy-start | bytes 6488068
  173.5 11.7 %slice-start.3 = ((s8[6291456]{0:T(1024)(128)(4,1)}), s8[2097152]{0:T(1024)(128)(4,1)S(1)}, s32[]{:S(2)}) async-start(s8[6291456]{0:T(1024)(128)(4,1)} %bitcast.215), calls=%async_computation.3 | async-start | bytes 4194304
  179.2 6.0 %slice-start.4 = ((s8[6291456]{0:T(1024)(128)(4,1)}), s8[4194304]{0:T(1024)(128)(4,1)S(1)}, s32[]{:S(2)}) async-start(s8[6291456]{0:T(1024)(128)(4,1)} %bitcast.215), calls=%async_computation.4 | async-start | bytes 8388608
  182.8 2.4 copy-start.34
  182.8 2.4 copy-start.36
  182.8 2.4 copy-start.38
  205.2 6.4 %copy-start.23 = (bf16[2,176,768]{2,1,0:T(8,128)(2,1)S(1)}, bf16[2,176,768]{2,1,0:T(8,128)(2,1)}, u32[]{:S(2)}) copy-start(bf16[2,176,768]{2,1,0:T(8,128)(2,1)} %get-tuple-element.39) | copy-start | bytes 1622020
  228.3 5.1 %copy-start.30 = (f32[2,6,2,256]{3,2,1,0:T(2,128)S(1)}, f32[2,6,2,256]{3,2,1,0:T(2,128)}, u32[]{:S(2)}) copy-start(f32[2,6,2,256]{3,2,1,0:T(2,128)} %get-tuple-element.42) | copy-start | bytes 73732
  233.5 3.0 copy-start.17
  236.5 2.3 copy-start.31
  236.9 2.4 copy-start.33
  239.4 3.2 copy-start.35
  242.5 3.0 copy-start.32
  245.6 3.4 copy-start.8
  245.6 3.4 copy-start.37
  245.6 3.4 copy-start.39
  269.0 2.1 copy-start.22
  271.1 1.8 copy-start.24
  274.9 2.2 copy-start.21
  438.5 2.8 copy-start.18
  443.1 2.4 copy-start.13
  447.4 2.5 copy-start.12
  451.6 2.6 copy-start.1
  (13 other events, 17.4 us)
where the time goes:
time: 459 us; the launch traced here: 454 us
  Pallas kernels  314 us (68%)
  matrix products  66.3 us (14%)
  local copies, waits for them, and re-layouts  44.4 us (10%)
  other arithmetic  28.6 us (6%)
    pallas_call x1, Pallas kernels, reduce_all(): pl.pallas_call(reduce_body, in_specs=[in_place, in_place, held, held, hel...  157 us
    pallas_call x1, Pallas kernels, gather_all(): pl.pallas_call(gather_body, in_specs=[held, held, in_place, held], out_sp...  102 us
    pallas_call x2, Pallas kernels, attend_back(): pl.pallas_call(partial(attend_back_body, causal), grid=(count, pairs), in...  28.3 us
    pallas_call x2, Pallas kernels, attend(): pl.pallas_call(partial(attend_body, bias is not None), grid=(count, pairs...  26.4 us
    dot_general x7, matrix products, times_t(): jnp.einsum('rtd,cd->rtc', values, weight, preferred_element_type=wide)  24.5 us
    unnamed x110, local copies, waits for them, and re-layouts  20.3 us
    concatenate x1, other arithmetic, shards(): jnp.concatenate([weight_grad(grad_gate_up, normed_three), weight_grad(hid...  15.8 us
    dot_general x5, matrix products, weight_grad(): jnp.einsum('rtc,rtd->cd', grads, values, preferred_element_type=wide)  12.8 us

commit v1 on v0

--- a/solution.py
+++ b/solution.py
@@ -130,21 +130,37 @@
         k, rows = self.spot(quarter, core)
         return refs[self.is_ffn].at[k, rows]
 
-    def whole(self, refs, steps, quarter, core):
+    def shards(self, refs, quarter, core):
         k, rows = self.spot(quarter, core)
-        return refs[self.is_ffn].at[k, steps, rows]
+        if self.is_ffn:
+            return [refs[1].at[pl.ds(0, 2), rows], refs[1].at[pl.ds(2, 1), rows]]
+        return [refs[0].at[k, rows]]
+
+    def wholes(self, refs, steps, quarter, core):
+        k, rows = self.spot(quarter, core)
+        if self.is_ffn:
+            return [refs[1].at[:, steps, rows], refs[2].at[:, steps, rows]]
+        return [refs[0].at[k, steps, rows]]
+
+
+def between_ends(step, me, mem):
+    to = (me + step) % mem
+    return jnp.logical_and(me - to < mem - 1, to - me < mem - 1)
 
 
 def gather_body(
     attn_ref, ffn_ref, enc_ref, table_ref,
-    attn_out, ffn_out, memory_out, tables_out,
-    own_enc, local_sems, far_send, far_recv, enc_send, enc_recv, table_send, table_recv,
+    input_ref, normed_ref, gain_ref, dec_row_ref, dec_column_ref, enc_row_ref, spread_ref,
+    attn_out, in_out, down_out, memory_out,
+    qkv_out, self_mixed_out, self_weights_out, first_out, normed_out,
+    queries_out, sides_out, cross_mixed_out, cross_weights_out,
+    own_enc, tables_out, bias_ref, weights_ref, memory_ref, local_sems, load_sems, far_send, far_recv, enc_send, enc_recv, table_send, table_recv,
     flat_send, flat_recv, core_send, core_recv,
 ):
     place = Place()
     mem = place.mem
     shards = (attn_ref, ffn_ref)
-    wholes = (attn_out, ffn_out)
+    wholes = (attn_out, in_out, down_out)
     count = own_enc.shape[0]
     chunks = [Chunk(i, attn_ref.shape[1], ffn_ref.shape[1]) for i in range(4)]
     locals_in = pltpu.make_async_copy(
@@ -153,24 +169,46 @@
     locals_in.start()
     locals_out = [
         pltpu.make_async_copy(attn_ref, attn_out.at[:, 0], local_sems.at[1]),
-        pltpu.make_async_copy(ffn_ref, ffn_out.at[:, 0], local_sems.at[2]),
+        pltpu.make_async_copy(ffn_ref.at[pl.ds(0, 2)], in_out.at[:, 0], local_sems.at[2]),
+        pltpu.make_async_copy(ffn_ref.at[pl.ds(2, 1)], down_out.at[:, 0], local_sems.at[3]),
     ]
     for copy in locals_out:
         copy.start()
     tables_out[0] = table_ref[...]
     place.greet()
     sent = []
+    waits = []
 
     def start_far(i):
+        sources = chunks[i].shards(shards, place.quarter, place.core)
         for step in range(1, mem):
             back = mem - step
-            sent.append(
-                send(
-                    chunks[i].shard(shards, place.quarter, place.core),
-                    chunks[i].whole(wholes, back, place.quarter, place.core),
-                    (far_send.at[i], far_recv.at[i]), step, place.along(step), back,
+            targets = chunks[i].wholes(wholes, back, place.quarter, place.core)
+            for j, (source, target) in enumerate(zip(sources, targets)):
+                copy = pltpu.make_async_remote_copy(
+                    src_ref=source, dst_ref=target,
+                    send_sem=far_send.at[i, 2 * step + j], recv_sem=far_recv.at[i, 2 * back + j],
+                    device_id=place.along(step), device_id_type=MESH,
                 )
-            )
+                direct = between_ends(step, place.me, mem)
+                pl.when(direct)(copy.start)
+                waits.append((direct, copy))
+
+    def relay(i):
+        for step, ahead in ((mem - 2, 1), (2, mem - 1)):
+            there = (step - ahead) % mem
+            at_turn = place.me == (mem - 2 if ahead == 1 else 1)
+            sources = chunks[i].wholes(wholes, step, place.quarter, place.core)
+            targets = chunks[i].wholes(wholes, there, place.quarter, place.core)
+            for j, (source, target) in enumerate(zip(sources, targets)):
+                copy = pltpu.make_async_remote_copy(
+                    src_ref=source, dst_ref=target,
+                    send_sem=far_send.at[i, 2 * mem + (ahead > 1) * 2 + j],
+                    recv_sem=far_recv.at[i, 2 * there + j],
+                    device_id=place.along(ahead), device_id_type=MESH,
+                )
+                pl.when(at_turn)(copy.start)
+                waits.append((at_turn, copy))
 
     def start_enc():
         for step in range(1, mem):
@@ -183,84 +221,216 @@
                 )
             )
 
+    def pieces(i, turn, core):
+        return enumerate(chunks[i].wholes(wholes, pl.ds(1, mem - 1), place.turn(turn), core))
+
     def pass_on(i, turn):
-        piece = chunks[i].whole(wholes, pl.ds(1, mem - 1), place.turn(turn), place.core)
-        sent.append(send(piece, piece, (core_send.at[i], core_recv.at[i]), turn, place.other_core()))
+        for j, piece in pieces(i, turn, place.core):
+            sems = (core_send.at[i], core_recv.at[i])
+            sent.append(send(piece, piece, sems, 2 * turn + j, place.other_core()))
 
     def finish_flat(i):
         for turn in range(1, quarters):
-            piece = chunks[i].whole(wholes, pl.ds(1, mem - 1), place.turn(turn), place.core)
-            expect(piece, (flat_send.at[i], flat_recv.at[i]), turn, place)
+            for j, piece in pieces(i, turn, place.core):
+                expect(piece, (flat_send.at[i], flat_recv.at[i]), 2 * turn + j, place)
             pass_on(i, turn)
 
+    def pass_far(i):
+        for step in (2, mem - 1, 1) if mem == 4 else range(1, mem):
+            for j, piece in enumerate(chunks[i].wholes(wholes, step, place.quarter, place.core)):
+                expect(piece, far_sems_of(i), 2 * step + j, place)
+            if step == 2:
+                relay(i)
+        for j, piece in pieces(i, 0, place.core):
+            sems = (flat_send.at[i], flat_recv.at[i])
+            for turn in range(1, quarters):
+                sent.append(send(piece, piece, sems, 2 * turn + j, place.other_quarter(turn)))
+        pass_on(i, 0)
+
+    def far_sems_of(i):
+        return far_send.at[i], far_recv.at[i]
+
+    def finish_core(i):
+        for turn in range(quarters):
+            for j, piece in pieces(i, turn, 1 - place.core):
+                expect(piece, (core_send.at[i], core_recv.at[i]), 2 * turn + j, place)
+
+    def bring(source, target):
+        copy = pltpu.make_async_copy(source, target, load_sems.at[0])
+        copy.start()
+        copy.wait()
+
+    def weight(k):
+        return weights_ref[k].reshape(-1, model)
+
+    model = attn_ref.shape[2]
+    rows, dec_len, _ = input_ref.shape
+    enc_len = mem * memory_ref.shape[2]
+    pairs = model // pair
+    own_heads = model // head_size // mem
+
+    start_far(0)
     for step in range(1, mem):
         back = mem - step
         sent.append(
             send(table_ref, tables_out.at[back], (table_send, table_recv), step, place.along(step), back)
         )
-    start_far(0)
-    start_far(1)
-    for i in range(4):
-        for step in range(1, mem):
-            piece = chunks[i].whole(wholes, step, place.quarter, place.core)
-            expect(piece, (far_send.at[i], far_recv.at[i]), step, place)
-        if i + 2 < 4:
-            start_far(i + 2)
-        if i == 2:
-            start_enc()
-        piece = chunks[i].whole(wholes, pl.ds(1, mem - 1), place.quarter, place.core)
-        for turn in range(1, quarters):
-            sent.append(
-                send(piece, piece, (flat_send.at[i], flat_recv.at[i]), turn, place.other_quarter(turn))
-            )
-        pass_on(i, 0)
-        if i > 0:
-            finish_flat(i - 1)
-    finish_flat(3)
+    for i in range(1, 4):
+        start_far(i)
+    pass_far(0)
+    for step in range(1, mem):
+        expect(tables_out.at[step], (table_send, table_recv), step, place)
+    for step in range(mem):
+        per_lane = dot(tables_out[step], spread_ref[...], 0, 0)
+        for head in range(own_heads):
+            bias_ref[step * own_heads + head] = per_lane[head : head + 1]
+    pass_far(1)
+    start_enc()
+    finish_flat(0)
+    pass_far(2)
+    finish_core(0)
+    for copy in locals_out:
+        copy.wait()
+    bring(attn_out.at[pl.ds(0, quarters)], weights_ref)
+
+    def project_self(k, carry):
+        values = dot(normed_ref[...].reshape(-1, model), weight(k), 1, 1)
+        qkv_out[k] = values.astype(low).reshape(rows, dec_len, model)
+        return carry
+
+    lax.fori_loop(0, 3, project_self, 0)
+    pass_far(3)
+
+    def lanes_at(p):
+        return pl.ds(pl.multiple_of(p * pair, pair), pair)
+
+    def self_row(r):
+        allowed = causal_mask(dec_column_ref[r] == dec_row_ref[r])
+
+        def step(p, carry):
+            weights, mixed = attend_pair(
+                qkv_out[0, r, :, lanes_at(p)],
+                qkv_out[1, r, :, lanes_at(p)],
+                qkv_out[2, r, :, lanes_at(p)],
+                allowed,
+                [bias_ref[2 * p], bias_ref[2 * p + 1]],
+            )
+            for half in range(2):
+                self_weights_out[r, 2 * p + half] = weights[half]
+            self_mixed_out[r, :, lanes_at(p)] = mixed
+            return carry
+
+        lax.fori_loop(0, pairs, step, 0)
+
+    def cross_row(r):
+        allowed = dec_column_ref[r] == enc_row_ref[r]
+
+        def step(p, carry):
+            weights, mixed = attend_pair(
+                queries_out[r, :, lanes_at(p)],
+                sides_out[0, r, :, lanes_at(p)],
+                sides_out[1, r, :, lanes_at(p)],
+                allowed,
+                None,
+            )
+            for half in range(2):
+                cross_weights_out[r, 2 * p + half] = weights[half]
+            cross_mixed_out[r, :, lanes_at(p)] = mixed
+            return carry
+
+        lax.fori_loop(0, pairs, step, 0)
+
+    for r in range(rows):
+        self_row(r)
+    finish_flat(1)
+    added = dot(self_mixed_out[...].reshape(-1, model), weight(3), 1, 0)
+    first = input_ref[...].astype(wide) + added.reshape(rows, dec_len, model)
+    first_out[...] = first
+    normed_out[...] = rms(first, gain_ref[1:2, :])[0]
+    finish_core(1)
+    bring(attn_out.at[pl.ds(quarters, quarters)], weights_ref)
+    values = dot(normed_out[...].reshape(-1, model), weight(0), 1, 1)
+    queries_out[...] = values.astype(low).reshape(rows, dec_len, model)
+    finish_flat(2)
     locals_in.wait()
     own_out = pltpu.make_async_copy(own_enc, memory_out.at[:, 0], local_sems.at[0])
     own_out.start()
-    for i in range(4):
-        for turn in range(quarters):
-            piece = chunks[i].whole(wholes, pl.ds(1, mem - 1), place.turn(turn), 1 - place.core)
-            expect(piece, (core_send.at[i], core_recv.at[i]), turn, place)
     for step in range(1, mem):
         expect(memory_out.at[:, step], (enc_send, enc_recv), step, place)
-        expect(tables_out.at[step], (table_send, table_recv), step, place)
+    own_out.wait()
+    bring(memory_out, memory_ref)
+    for k in range(2):
+
+        def project_side(r, carry):
+            values = dot(memory_ref[r].reshape(-1, model), weight(1 + k), 1, 1)
+            sides_out[k, r] = values.astype(low)
+            return carry
+
+        lax.fori_loop(0, rows, project_side, 0)
+    cross_row(0)
+    finish_flat(3)
+    for r in range(1, rows):
+        cross_row(r)
+    finish_core(2)
+    finish_core(3)
     for copy in sent:
         copy.wait_send()
-    for copy in locals_out:
-        copy.wait()
-    own_out.wait()
-
-
-def gather_all(attn, ffn, enc, table):
+    for started, copy in waits:
+        pl.when(started)(copy.wait_send)
+
+
+def gather_all(attn, ffn, enc, table, inputs, normed, gains, dec_ids, enc_ids, spread):
     mem = lax.axis_size("mem")
-    count = enc.shape[0] // mem
+    count, dec_len, model = inputs.shape
+    enc_len = enc_ids.shape[1]
+    heads = model // head_size
     dma = pltpu.SemaphoreType.DMA
     in_place = pl.BlockSpec(memory_space=pl.ANY)
     held = pl.BlockSpec(memory_space=pltpu.VMEM)
+    operands = (
+        attn, ffn, enc, table, inputs, normed, gains,
+        dec_ids[:, None, :], dec_ids[:, :, None], enc_ids[:, None, :], spread,
+    )
+
+    def values(*shape, dtype=low):
+        return jax.ShapeDtypeStruct(shape, dtype)
+
     return pl.pallas_call(
         gather_body,
-        in_specs=[held, held, in_place, held],
-        out_specs=[in_place, in_place, in_place, held],
+        in_specs=[held, held, in_place] + [held] * (len(operands) - 3),
+        out_specs=[in_place] * 4 + [held] * 9,
         out_shape=[
-            jax.ShapeDtypeStruct((attn.shape[0], mem) + attn.shape[1:], low),
-            jax.ShapeDtypeStruct((ffn.shape[0], mem) + ffn.shape[1:], low),
-            jax.ShapeDtypeStruct((count, mem) + enc.shape[1:], low),
-            jax.ShapeDtypeStruct((mem,) + table.shape, low),
+            values(attn.shape[0], mem, *attn.shape[1:]),
+            values(2, mem, *ffn.shape[1:]),
+            values(1, mem, *ffn.shape[1:]),
+            values(count, mem, *enc.shape[1:]),
+            values(3, count, dec_len, model),
+            values(count, dec_len, model),
+            values(count, heads, dec_len, dec_len),
+            values(count, dec_len, model, dtype=wide),
+            values(count, dec_len, model),
+            values(count, dec_len, model),
+            values(2, count, enc_len, model),
+            values(count, dec_len, model),
+            values(count, heads, dec_len, enc_len),
         ],
         scratch_shapes=[
             pltpu.VMEM((count,) + enc.shape[1:], low),
-            dma((3,)),
-            dma((4, mem)), dma((4, mem)),
+            pltpu.VMEM((mem,) + table.shape, low),
+            pltpu.VMEM((heads, 1, spread.shape[1]), wide),
+            pltpu.VMEM((quarters, mem) + attn.shape[1:], low),
+            pltpu.VMEM((count, mem) + enc.shape[1:], low),
+            dma((4,)), dma((1,)),
+            dma((4, 2 * mem + 4)), dma((4, 2 * mem)),
             dma((mem,)), dma((mem,)),
             dma((mem,)), dma((mem,)),
-            dma((4, quarters)), dma((4, quarters)),
-            dma((4, quarters)), dma((4, quarters)),
+            dma((4, 2 * quarters)), dma((4, 2 * quarters)),
+            dma((4, 2 * quarters)), dma((4, 2 * quarters)),
         ],
-        compiler_params=pltpu.CompilerParams(collective_id=0, has_side_effects=True),
-    )(attn, ffn, enc, table)
+        compiler_params=pltpu.CompilerParams(
+            collective_id=0, has_side_effects=True, vmem_limit_bytes=60000000
+        ),
+    )(*operands)
 
 
 def add_planes(total_ref, total_at, more_ref, more_at, k, steps):
@@ -277,7 +447,8 @@
 
 
 def reduce_body(
-    attn_ref, ffn_ref, memory_ref, first_ref, second_ref, small_ref,
+    qkv_ref, self_out_ref, query_ref, kv_ref, cross_out_ref, in_ref, down_ref,
+    memory_ref, first_ref, second_ref, small_ref,
     attn_out, ffn_out, memory_out, first_out, second_out, small_out,
     held_attn, held_ffn, core_attn, core_ffn, near_attn, near_ffn, last_attn, last_ffn,
     far_attn, far_ffn, small_far, small_flat,
@@ -288,7 +459,8 @@
     place = Place()
     mem = place.mem
     half = mem // 2
-    grads = (attn_ref, ffn_ref)
+    attn_grads = [(qkv_ref, 0), (qkv_ref, 1), (qkv_ref, 2), (self_out_ref, 0)]
+    attn_grads += [(query_ref, 0), (kv_ref, 0), (kv_ref, 1), (cross_out_ref, 0)]
     outs = (attn_out, ffn_out)
     chunks = [Chunk(i, attn_out.shape[1], ffn_out.shape[1]) for i in range(4)]
     helds = (held_attn, held_ffn)
@@ -305,32 +477,50 @@
         kind, part = chunks[i].is_ffn, chunks[i].part
         return tuple(group[kind].at[part] for group in (helds, cores, nears, lasts, fars))
 
+    def parts_of(i, quarter, core):
+        k, rows = chunks[i].spot(quarter, core)
+        if chunks[i].is_ffn:
+            yield in_ref.at[:, :, rows], 0, 2
+            yield down_ref.at[:, :, rows], 2, 1
+        else:
+            ref, at = attn_grads[chunks[i].part * quarters + quarter]
+            yield ref.at[pl.ds(at, 1), :, rows], 0, 1
+
     def load(i):
-        held, core = buffers(i)[:2]
+        held = buffers(i)[0]
         for quarter in range(quarters):
-            copy = pltpu.make_async_copy(
-                chunks[i].whole(grads, pl.ds(0, mem), quarter, place.core),
-                held.at[quarter], local_sems.at[i, quarter],
-            )
-            copy.start()
-            loads[i, quarter] = copy
+            loads[i, quarter] = []
+            for source, first, planes in parts_of(i, quarter, place.core):
+                copy = pltpu.make_async_copy(
+                    source, held.at[quarter, pl.ds(first, planes)],
+                    local_sems.at[i, quarter + first // 2 * quarters],
+                )
+                copy.start()
+                loads[i, quarter].append(copy)
 
     def to_core(i):
         core = buffers(i)[1]
         for quarter in range(quarters):
-            sent.append(
-                send(
-                    chunks[i].whole(grads, pl.ds(0, mem), quarter, 1 - place.core),
-                    core.at[quarter], (core_send.at[i], core_recv.at[i]), quarter,
-                    place.other_core(),
+            for source, first, planes in parts_of(i, quarter, 1 - place.core):
+                sent.append(
+                    send(
+                        source, core.at[quarter, pl.ds(first, planes)],
+                        (core_send.at[i], core_recv.at[i]), quarter + first // 2 * quarters,
+                        place.other_core(),
+                    )
                 )
-            )
 
     def from_core(i):
         held, core, near = buffers(i)[:3]
         for quarter in range(quarters):
-            loads[i, quarter].wait()
-            expect(core.at[quarter], (core_send.at[i], core_recv.at[i]), quarter, place)
+            for copy in loads[i, quarter]:
+                copy.wait()
+            sems = (core_send.at[i], core_recv.at[i])
+            if chunks[i].is_ffn:
+                expect(core.at[quarter, pl.ds(0, 2)], sems, quarter, place)
+                expect(core.at[quarter, pl.ds(2, 1)], sems, quarter + quarters, place)
+            else:
+                expect(core.at[quarter], sems, quarter, place)
             add_planes(held, (quarter,), core, (quarter,), chunks[i].k, (0, mem))
         sems = (near_send.at[i], near_recv.at[i])
         for bit in range(2):
@@ -444,7 +634,7 @@
         )
     phases = (from_core, from_near, from_last, from_far, from_flat, from_pass)
     for time in range(len(order) + len(phases) - 1):
-        for slot, i in enumerate(order):
+        for slot, i in reversed(list(enumerate(order))):
             if 0 <= time - slot < len(phases):
                 phases[time - slot](i)
         if time == 1:
@@ -477,11 +667,14 @@
 
 def reduce_all(attn, ffn, memory, first, second, small):
     mem = lax.axis_size("mem")
-    model = attn.shape[-1]
+    own_width, model = attn[0].shape[-2:]
+    own_hidden = ffn[0].shape[-2]
+    attn_count = sum(grad.shape[0] for grad in attn)
+    ffn_count = sum(grad.shape[0] for grad in ffn)
     dma = pltpu.SemaphoreType.DMA
     in_place = pl.BlockSpec(memory_space=pl.ANY)
     held = pl.BlockSpec(memory_space=pltpu.VMEM)
-    chunks = [Chunk(i, attn.shape[2], ffn.shape[2]) for i in (0, 2)]
+    chunks = [Chunk(i, own_width, own_hidden) for i in (0, 2)]
 
     def both(*shape_of):
         return [
@@ -495,17 +688,17 @@
     def rows(chunk):
         return chunk.rows
 
-    sem_shapes = ((4, quarters), (4, quarters), (4, 2), (4, mem), (4, quarters), (4, quarters), (3, mem), (mem + block,))
-    sems = [dma((5, quarters))]
+    sem_shapes = ((4, 2 * quarters), (4, quarters), (4, 2), (4, mem), (4, quarters), (4, quarters), (3, mem), (mem + block,))
+    sems = [dma((5, 2 * quarters))]
     for shape in sem_shapes:
         sems += [dma(shape), dma(shape)]
     return pl.pallas_call(
         reduce_body,
-        in_specs=[in_place, in_place, held, held, held, held],
+        in_specs=[in_place] * (len(attn) + len(ffn)) + [held, held, held, held],
         out_specs=[held, held, in_place, in_place, in_place, held],
         out_shape=[
-            jax.ShapeDtypeStruct((attn.shape[0],) + attn.shape[2:], low),
-            jax.ShapeDtypeStruct((ffn.shape[0],) + ffn.shape[2:], low),
+            jax.ShapeDtypeStruct((attn_count, own_width, model), low),
+            jax.ShapeDtypeStruct((ffn_count, own_hidden, model), low),
             jax.ShapeDtypeStruct((mem, memory.shape[0]) + memory.shape[2:], low),
             jax.ShapeDtypeStruct(first.shape, low),
             jax.ShapeDtypeStruct(second.shape, low),
@@ -519,7 +712,7 @@
         + [pltpu.VMEM((mem,) + small.shape[1:], wide), pltpu.VMEM((block,) + small.shape[1:], wide)]
         + sems,
         compiler_params=pltpu.CompilerParams(collective_id=1, has_side_effects=True),
-    )(attn, ffn, memory, first, second, small)
+    )(*attn, *ffn, memory, first, second, small)
 
 
 def sum_blocks(values):
@@ -546,31 +739,29 @@
     return pltpu.roll(spread, 0, 1, stride=1, stride_axis=0)
 
 
-def attend_body(causal, q_ref, k_ref, v_ref, dec_ref, key_ref, *rest):
-    if causal:
-        bias_ref, out_ref, weight_ref = rest
-    else:
-        out_ref, weight_ref = rest
-    queries, keys_in, values_in = q_ref[0], k_ref[0], v_ref[0]
-    rows, keys = queries.shape[0], keys_in.shape[0]
-    allowed = dec_ref[0] == key_ref[0]
-    if causal:
-        i = lax.broadcasted_iota(jnp.int32, (rows, keys), 0)
-        j = lax.broadcasted_iota(jnp.int32, (rows, keys), 1)
-        allowed = allowed & (i >= j)
+def causal_mask(same):
+    rows, keys = same.shape
+    i = lax.broadcasted_iota(jnp.int32, (rows, keys), 0)
+    j = lax.broadcasted_iota(jnp.int32, (rows, keys), 1)
+    return same & (i >= j)
+
+
+def attend_pair(queries, keys_in, values_in, allowed, bias):
+    rows, keys = allowed.shape
+    kept = []
     mixed = jnp.zeros((rows, pair), wide)
     for half in range(2):
         lanes = lanes_of(half)
         scores = dot(queries * lanes.astype(low), keys_in, 1, 1)
-        if causal:
-            scores = scores + skewed(bias_ref[0, half : half + 1, :], rows)[:, :keys]
+        if bias is not None:
+            scores = scores + skewed(bias[half], rows)[:, :keys]
         scores = jnp.where(allowed, scores, negative)
         raised = jnp.exp(scores - jnp.max(scores, axis=-1, keepdims=True))
         scale = 1.0 / jnp.sum(raised, axis=-1, keepdims=True)
         weights = (raised * scale).astype(low)
-        weight_ref[0, half] = weights
+        kept.append(weights)
         mixed = mixed + dot(weights, values_in, 1, 0) * lanes
-    out_ref[0] = mixed.astype(low)
+    return kept, mixed.astype(low)
 
 
 def attend_back_body(causal, w_ref, q_ref, k_ref, v_ref, g_ref, *rest):
@@ -613,8 +804,10 @@
         dkv_ref[0, 1] = dv.astype(low)
 
 
-def column(length, offset):
-    return pl.BlockSpec((1, length, pair), lambda r, p: (r, 0, p + offset))
+def column(length, k=None):
+    if k is None:
+        return pl.BlockSpec((1, length, pair), lambda r, p: (r, 0, p))
+    return pl.BlockSpec((None, 1, length, pair), lambda r, p: (k, r, 0, p))
 
 
 def cost_of(count, rows, keys, pairs, dots):
@@ -625,43 +818,7 @@
     )
 
 
-def whole_row(*shape):
-    return pl.BlockSpec((1,) + shape, lambda r, p: (r,) + (0,) * len(shape))
-
-
-def attend(queries, sides, offsets, dec_ids, key_ids, bias):
-    count, rows, _ = queries.shape
-    keys = sides.shape[1]
-    pairs = queries.shape[2] // pair if bias is None else bias.shape[0]
-    width = pairs * pair
-    in_specs = [
-        column(rows, 0),
-        column(keys, offsets[0]),
-        column(keys, offsets[1]),
-        whole_row(rows, 1),
-        whole_row(1, keys),
-    ]
-    operands = [queries, sides, sides, dec_ids[:, :, None], key_ids[:, None, :]]
-    if bias is not None:
-        in_specs.append(pl.BlockSpec((1, 2, bias.shape[2]), lambda r, p: (p, 0, 0)))
-        operands.append(bias)
-    return pl.pallas_call(
-        partial(attend_body, bias is not None),
-        grid=(count, pairs),
-        in_specs=in_specs,
-        out_specs=[
-            column(rows, 0),
-            pl.BlockSpec((1, 2, rows, keys), lambda r, p: (r, p, 0, 0)),
-        ],
-        out_shape=[
-            jax.ShapeDtypeStruct((count, rows, width), low),
-            jax.ShapeDtypeStruct((count, pairs * 2, rows, keys), low),
-        ],
-        cost_estimate=cost_of(count, rows, keys, pairs, 2),
-    )(*operands)
-
-
-def attend_back(weights, queries, sides, offsets, grad, dist_width):
+def attend_back(weights, queries, keys_in, values_in, grad, dist_width):
     count, heads, rows, keys = weights.shape
     pairs = heads // 2
     width = pairs * pair
@@ -677,7 +834,7 @@
         ]
     else:
         out_specs = [
-            column(rows, 0),
+            column(rows),
             pl.BlockSpec((1, 2, keys, pair), lambda r, p: (r, 0, 0, p)),
         ]
         out_shape = [
@@ -689,15 +846,15 @@
         grid=(count, pairs),
         in_specs=[
             pl.BlockSpec((1, 2, rows, keys), lambda r, p: (r, p, 0, 0)),
-            column(rows, 0),
-            column(keys, offsets[0]),
-            column(keys, offsets[1]),
-            column(rows, 0),
+            column(rows, queries[1]),
+            column(keys, keys_in[1]),
+            column(keys, values_in[1]),
+            column(rows),
         ],
         out_specs=out_specs,
         out_shape=out_shape,
         cost_estimate=cost_of(count, rows, keys, pairs, 4),
-    )(weights, queries, sides, sides, grad)
+    )(weights, queries[0], keys_in[0], values_in[0], grad)
 
 
 def rms(values, gain):
@@ -764,21 +921,16 @@
     )
     ffn_shard = jnp.stack([ffn_in[0].T, ffn_in[1].T, ffn_out])
     padded_table = jnp.pad(rel_table, ((0, 0), (0, pair - own_heads)))
-    attn_weights, ffn_weights, memory, tables = gather_all(
-        attn_shard, ffn_shard, enc_output, padded_table
-    )
-    attn_weights = attn_weights.reshape(-1, width, model)
-    ffn_weights = ffn_weights.reshape(-1, model)
-    memory = memory.reshape(count, -1, model)
 
     def mine(values):
         return lax.dynamic_slice_in_dim(values, me * count, count, 0)
 
-    inputs = mine(dec_input).astype(wide)
+    own_input = mine(dec_input)
+    inputs = own_input.astype(wide)
     grad_out = mine(cotangent)
     dec_ids = mine(dec_segments)
     enc_ids = jnp.concatenate(relative(mine(enc_segments), 1, mem), axis=1)
-    enc_len = memory.shape[1]
+    enc_len = enc_ids.shape[1]
 
     lane_count = -(-dec_len // pair) * pair
     turned = jnp.concatenate(
@@ -788,37 +940,31 @@
             jnp.flip(buckets[1:]),
         ]
     )
-    def one_hot_of(ids):
-        return (ids[:, None] == jnp.arange(bucket_count)[None, :]).astype(wide)
-
-    one_hot = one_hot_of(turned)
-    table = tables[:, :, :own_heads].astype(wide)
-    bias = jnp.einsum("mbh,lb->mhl", table, one_hot, precision=highest)
-    bias = bias.reshape(pairs, 2, lane_count)
-
-    qkv_weight = attn_weights[:3].reshape(3 * width, model)
+    spread = (jnp.arange(bucket_count)[:, None] == turned[None, :]).astype(low)
+
+    normed_one, scale_one = rms(inputs, gain_values[0])
+    (
+        attn_weights, in_weight, out_weight, memory,
+        qkv, self_mixed, self_weights, first, normed_two,
+        cross_queries, cross_sides, cross_mixed, cross_weights,
+    ) = gather_all(
+        attn_shard, ffn_shard, enc_output, padded_table,
+        own_input, normed_one, gain_values, dec_ids, enc_ids, spread,
+    )
+    attn_weights = attn_weights.reshape(-1, width, model)
+    in_weight = in_weight.reshape(-1, model)
+    out_weight = out_weight.reshape(-1, model)
+    memory = memory.reshape(count, -1, model)
+    qkv_weight = attn_weights[:3]
     self_out_weight = attn_weights[3]
     cross_query_weight = attn_weights[4]
-    cross_kv_weight = attn_weights[5:7].reshape(2 * width, model)
+    cross_kv_weight = attn_weights[5:7]
     cross_out_weight = attn_weights[7]
-    normed_one, scale_one = rms(inputs, gain_values[0])
-    qkv = times_t(normed_one, qkv_weight).astype(low)
-    self_mixed, self_weights = attend(
-        qkv, qkv, (pairs, 2 * pairs), dec_ids, dec_ids, bias
-    )
-    first = inputs + times(self_mixed, self_out_weight)
-    normed_two, scale_two = rms(first, gain_values[1])
-    cross_kv_values = times_t(memory, cross_kv_weight).astype(low)
-    cross_queries = times_t(normed_two, cross_query_weight).astype(low)
-    cross_mixed, cross_weights = attend(
-        cross_queries, cross_kv_values, (0, pairs), dec_ids, enc_ids, None
-    )
+    scale_two = rms(first, gain_values[1])[1]
     second = first + times(cross_mixed, cross_out_weight)
     normed_three, scale_three = rms(second, gain_values[2])
 
     hidden_width = mem * own_hidden
-    in_weight = ffn_weights[: 2 * hidden_width]
-    out_weight = ffn_weights[2 * hidden_width :]
     gate_up = times_t(normed_three, in_weight)
     hidden_float, pull = jax.vjp(gated, gate_up[..., :hidden_width], gate_up[..., hidden_width:])
     hidden = hidden_float.astype(low)
@@ -826,9 +972,10 @@
     grad_gate, grad_up = pull(times_t(grad_out, out_weight))
     grad_gate_up = jnp.concatenate([grad_gate.astype(low), grad_up.astype(low)], axis=-1)
     grad_three = times(grad_gate_up, in_weight)
-    ffn_grads = jnp.concatenate(
-        [weight_grad(grad_gate_up, normed_three), weight_grad(hidden, grad_out)]
-    ).reshape(3, mem, own_hidden, model)
+    ffn_grads = [
+        grad.reshape(-1, mem, own_hidden, model)
+        for grad in (weight_grad(grad_gate_up, normed_three), weight_grad(hidden, grad_out))
+    ]
 
     grad_wide = grad_out.astype(wide)
     back, gain_three = rms_back(second, scale_three, gain_values[2], grad_three)
@@ -837,7 +984,12 @@
     grad_cross_mixed = times_t(grad_second_low, cross_out_weight).astype(low)
     grad_cross_out = weight_grad(cross_mixed, grad_second_low)
     cross_dq, cross_dkv = attend_back(
-        cross_weights, cross_queries, cross_kv_values, (0, pairs), grad_cross_mixed, None
+        cross_weights,
+        (cross_queries, None),
+        (cross_sides, 0),
+        (cross_sides, 1),
+        grad_cross_mixed,
+        None,
     )
     grad_cross_query = weight_grad(cross_dq, normed_two)
     grad_cross_kv = jnp.einsum(
@@ -846,7 +998,7 @@
     grad_memory = jnp.einsum(
         "rmsc,mcd->rsd",
         cross_dkv,
-        cross_kv_weight.reshape(2, width, model),
+        cross_kv_weight,
         preferred_element_type=wide,
     ).astype(low)
     back, gain_two = rms_back(
@@ -857,28 +1009,26 @@
     grad_self_mixed = times_t(grad_first_low, self_out_weight).astype(low)
     grad_self_out = weight_grad(self_mixed, grad_first_low)
     self_grads, distance_sums = attend_back(
-        self_weights, qkv, qkv, (pairs, 2 * pairs), grad_self_mixed, lane_count
+        self_weights, (qkv, 0), (qkv, 1), (qkv, 2), grad_self_mixed, lane_count
     )
     grad_qkv = jnp.einsum(
         "rmtc,rtd->mcd", self_grads, normed_one, preferred_element_type=wide
     ).astype(low)
-    attn_grads = jnp.concatenate(
-        [
-            grad_qkv.reshape(3 * width, model),
-            grad_self_out,
-            grad_cross_query,
-            grad_cross_kv.reshape(2 * width, model),
-            grad_cross_out,
-        ]
-    ).reshape(8, mem, own_width, model)
+    attn_grads = [
+        grad.reshape(-1, mem, own_width, model)
+        for grad in (grad_qkv, grad_self_out, grad_cross_query, grad_cross_kv, grad_cross_out)
+    ]
     grad_one = jnp.einsum(
         "rmtc,mcd->rtd",
         self_grads,
-        qkv_weight.reshape(3, width, model),
+        qkv_weight,
         preferred_element_type=wide,
     )
     back, gain_one = rms_back(inputs, scale_one, gain_values[0], grad_one)
     grad_input = grad_first + back
+
+    def one_hot_of(ids):
+        return (ids[:, None] == jnp.arange(bucket_count)[None, :]).astype(wide)
 
     falling = jnp.concatenate(
         [jnp.flip(buckets), jnp.full((lane_count - dec_len,), -1, buckets.dtype)]

time: 459 us -> 401 us (0.87)
  Pallas kernels: 314 us -> 291 us
  matrix products: 66.3 us -> 49.7 us
  other arithmetic: 28.6 us -> 14.4 us
    pallas_call x4 -> x2, Pallas kernels: 285 us -> 262 us  [the longest x1 148 us: reduce_all(): pl.pallas_call(reduce_body, in_specs=[in_place] * (len(attn) + len(ffn))...]
    concatenate x1 -> x0, other arithmetic: 15.8 us -> none  [shards(): jnp.concatenate([weight_grad(grad_gate_up, normed_three), weight_grad(hid...]
    dot_general x7 -> x4, matrix products: 24.5 us -> 8.84 us  [times_t(): jnp.einsum('rtd,cd->rtc', values, weight, preferred_element_type=wide)]
    unnamed x110, local copies, waits for them, and re-layouts: 20.3 us -> 15.4 us
    dot_general x5 -> x4, matrix products: 9.79 us -> 6.25 us  [times(): jnp.einsum('rtc,cd->rtd', values, weight, preferred_element_type=wide)]
    slice x6 -> x4, local copies, waits for them, and re-layouts: 8.69 us -> 11.2 us  [the longest x1 4.16 us: shards(): qkv_weight = attn_weights[:3]]
    dot_general x3 -> x2, matrix products: 12.5 us -> 10.1 us  [the longest x1 6.48 us: shards(): jnp.einsum('rmsc,mcd->rsd', cross_dkv, cross_kv_weight, preferred_element...]
where the time goes in v1:
time: 401 us; the launch traced here: 396 us
  Pallas kernels  291 us (73%)
  matrix products  49.7 us (12%)
  local copies, waits for them, and re-layouts  40 us (10%)
  other arithmetic  14.4 us (4%)
    pallas_call x1, Pallas kernels, reduce_all(): pl.pallas_call(reduce_body, in_specs=[in_place] * (len(attn) + len(ffn))...  148 us
    pallas_call x1, Pallas kernels, gather_all(): pl.pallas_call(gather_body, in_specs=[held, held, in_place] + [held] * (l...  114 us
    pallas_call x2, Pallas kernels, attend_back(): pl.pallas_call(partial(attend_back_body, causal), grid=(count, pairs), in...  28.3 us
    dot_general x5, matrix products, weight_grad(): jnp.einsum('rtc,rtd->cd', grads, values, preferred_element_type=wide)  16.4 us
    unnamed x110, local copies, waits for them, and re-layouts  15.4 us
    dot_general x4, matrix products, times_t(): jnp.einsum('rtd,cd->rtc', values, weight, preferred_element_type=wide)  8.84 us

profile of v1, /device:TPU:25, one launch (start us, length us, event | category | flops | bytes accessed | tf_op | source)
XLA Modules:
  0.0 396.3 jit_solution(3521626721341634652)
XLA Ops:
  13.7 1.7 pad_maximum_fusion.1.ffn_ref
  16.7 1.4 copy-done.9
  18.1 114.0 %shard_map.255 = (bf16[8,4,192,768]{3,2,1,0:T(8,128)(2,1)}, bf16[2,4,512,768]{3,2,1,0:T(8,128)(2,1)}, bf16[1,4,512,768]{3,2,1,0:T(8,128)(2,1)}, bf16[2,4,128,768...) custom-call(bf16[8,192,768]{2,1,0:T(8,128)(2,1)} %copy-done.9, ...), custom_call_target="tpu_custom_call" | custom-call | tf_op jit(solution)/shard_map/pallas_call | solution.py:398
  132.1 1.4 multiply_reduce_fusion.3
  133.5 3.2 slice.114
  136.8 4.2 %slice.116 = bf16[3,4,192,768]{3,2,1,0:T(8,128)(2,1)} slice(bf16[8,4,192,768]{3,2,1,0:T(8,128)(2,1)} %get-tuple-element.41), slice={[0:3], [0:4], [0:192], [0:768]} | slice | bytes 7077888 | tf_op jit(solution)/shard_map/slice | solution.py:958
  140.9 3.8 fusion.38
  145.5 2.4 fusion.26
  148.4 3.5 fusion.6
  151.9 2.2 fusion.8
  154.1 2.6 multiply_reduce_fusion
  157.0 1.4 convolution_convert_fusion.1.g_ref
  158.5 14.6 %shard_map.256 = (bf16[2,176,768]{2,1,0:T(8,128)(2,1)}, bf16[2,2,512,768]{3,2,1,0:T(8,128)(2,1)}) custom-call(bf16[2,12,176,512]{3,2,1,0:T(8,128)(2,1)} %get-tuple-element.43.w_ref, bf16[2,176,768]{2,1,0:T(8,128)(2,1)} %get-tuple-element.44.q_ref, bf16[2,2,512,768]{3,2,1,0:T(8,128)(2,1)} %get-tuple-element.45.k_ref.v_ref, ...), custom_call_target="tpu_custom_call" | custom-call | flops 2214592512 | bytes 10616832 | tf_op jit(solution)/shard_map/pallas_call | solution.py:844
  173.1 6.5 %bitcast_convert_fusion.4 = bf16[2,512,768]{2,1,0:T(8,128)(2,1)} fusion(bf16[2,2,512,768]{3,2,1,0:T(8,128)(2,1)} %get-tuple-element.50, bf16[2,768,768,1]{2,1,0,3:T(8,128)(2,1)} %bitcast.199), kind=kOutput, calls=%fused_computation.7 | convolution fusion | flops 2416705536 | bytes 7077888 | tf_op jit(solution)/shard_map/rmsc,mcd->rsd/dot_general | solution.py:998
  181.7 1.4 convolution_convert_fusion.g_ref
  183.1 13.7 %shard_map.257 = (bf16[2,3,176,768]{3,2,1,0:T(8,128)(2,1)}, f32[2,6,2,256]{3,2,1,0:T(2,128)}) custom-call(bf16[2,12,176,176]{3,2,1,0:T(8,128)(2,1)} %get-tuple-element.36.w_ref, bf16[3,2,176,768]{3,2,1,0:T(8,128)(2,1)} %get-tuple-element.37.q_ref.k_ref.v_ref, bf16[3,2,176,768]{3,2,1,0:T(8,128)(2,1)} %get-tuple-element.37.q_ref.k_ref.v_ref, ...), custom_call_target="tpu_custom_call" | custom-call | flops 761266176 | bytes 3649536 | tf_op jit(solution)/shard_map/pallas_call | solution.py:844
  196.8 1.9 bitcast_convert_fusion.5
  198.7 3.6 fusion.17
  203.5 1.8 bitcast_convert_fusion.7
  207.9 1.8 bitcast_convert_fusion.6
  210.6 4.0 bitcast_convert_fusion.3
  214.6 4.7 %bitcast_convert_fusion.2 = bf16[2048,768]{1,0:T(8,128)(2,1)} fusion(bf16[2,176,2048]{2,1,0:T(8,128)(2,1)S(1)} %copy-done.39, bf16[8,176,768]{2,1,0:T(8,128)(2,1)} %param.31, s32[]{:T(128)S(6)} %select_n.99), kind=kOutput, calls=%fused_computation.2 | convolution fusion | flops 1108869120 | bytes 5128196 | tf_op jit(solution)/shard_map/rtc,rtd->cd/dot_general | solution.py:881
  219.4 6.1 %bitcast_convert_fusion = bf16[4096,768]{1,0:T(8,128)(2,1)} fusion(bf16[2,176,2048]{2,1,0:T(8,128)(2,1)S(1)} %copy-done.43, bf16[2,176,2048]{2,1,0:T(8,128)(2,1)S(1)} %copy-done.41, f32[2,176,768]{2,1,0:T(8,128)S(1)} %copy-done.8, f32[768]{0:T(1024)S(1)} %get-tuple-element.92, f32[2,176]{1,0:T(2,128)S(1)} %add_rsqrt_fusion.1), kind=kOutput, calls=%fused_computation | convolution fusion | flops 2224316416 | bytes 10260864 | tf_op jit(solution)/shard_map/rtc,rtd->cd/dot_general | solution.py:881
  225.5 3.9 bitcast_convert_fusion.1
  229.4 148.3 %shard_map.258 = (bf16[8,192,768]{2,1,0:T(8,128)(2,1)}, bf16[3,512,768]{2,1,0:T(8,128)(2,1)}, bf16[4,2,128,768]{3,2,1,0:T(8,128)(2,1)}, bf16[4,2,44,768]{3,2,1,0...) custom-call(bf16[3,4,192,768]{3,2,1,0:T(8,128)(2,1)} %bitcast.194, bf16[1,4,192,768]{3,2,1,0:T(8,128)(2,1)} %bitcast.202, ...), custom_call_target="tpu_custom_call" | custom-call | tf_op jit(solution)/shard_map/pallas_call | solution.py:695
  377.8 1.4 reshape.179
  381.6 1.6 copy.43
  383.4 1.6 copy.44
  385.0 2.0 bitcast_convert_fusion.8
  387.9 1.4 slice_bitcast_fusion.4
  389.3 1.6 slice_bitcast_fusion.2
  393.7 2.4 copy.45
  (161 shorter events, 28.5 us)
Async XLA Ops:
  0.6 5.3 %copy-start = (s32[8,176]{1,0:T(8,128)S(1)}, s32[8,176]{1,0:T(8,128)}, u32[]{:S(2)}) copy-start(s32[8,176]{1,0:T(8,128)} %param.18) | copy-start | bytes 16900
  8.6 3.9 copy-start.29
  10.1 2.4 copy-start.13
  13.7 1.7 copy-start.18
  136.8 8.7 %slice-start = ((s8[6291456]{0:T(1024)(128)(4,1)}), s8[4194304]{0:T(1024)(128)(4,1)S(1)}, s32[]{:S(2)}) async-start(s8[6291456]{0:T(1024)(128)(4,1)} %bitcast.209), calls=%async_computation | async-start | bytes 8388608
  140.9 3.8 copy-start.2
  140.9 3.8 copy-start.20
  140.9 4.5 %slice-start.1 = ((s8[6291456]{0:T(1024)(128)(4,1)}), s8[2097152]{0:T(1024)(128)(4,1)S(1)}, s32[]{:S(2)}) async-start(s8[6291456]{0:T(1024)(128)(4,1)} %bitcast.209), calls=%async_computation.1 | async-start | bytes 4194304
  145.4 11.3 %copy-start.7 = (f32[2,176,768]{2,1,0:T(8,128)}, f32[2,176,768]{2,1,0:T(8,128)S(1)}, u32[]{:S(2)}) copy-start(f32[2,176,768]{2,1,0:T(8,128)S(1)} %get-tuple-element.127) | copy-start | bytes 3244036
  145.5 2.5 copy-start.28
  145.5 2.9 copy-start.32
  151.9 2.2 copy-start.38
  151.9 2.2 copy-start.40
  151.9 2.2 copy-start.42
  173.1 6.5 %copy-start.5 = (bf16[1,4,192,768]{3,2,1,0:T(8,128)(2,1)S(1)}, bf16[1,4,192,768]{3,2,1,0:T(8,128)(2,1)}, u32[]{:S(2)}) copy-start(bf16[1,4,192,768]{3,2,1,0:T(8,128)(2,1)} %get-tuple-element.96) | copy-start | bytes 3538948
  173.1 6.5 %copy-start.22 = (bf16[2,176,768]{2,1,0:T(8,128)(2,1)S(1)}, bf16[2,176,768]{2,1,0:T(8,128)(2,1)}, u32[]{:S(2)}) copy-start(bf16[2,176,768]{2,1,0:T(8,128)(2,1)} %get-tuple-element.46) | copy-start | bytes 1622020
  183.1 13.7 %copy-start.21 = (bf16[2,176,768]{2,1,0:T(8,128)(2,1)S(1)}, bf16[2,176,768]{2,1,0:T(8,128)(2,1)}, u32[]{:S(2)}) copy-start(bf16[2,176,768]{2,1,0:T(8,128)(2,1)} %get-tuple-element.40) | copy-start | bytes 1622020
  196.8 1.9 copy-start.4
  196.8 1.9 copy-start.33
  198.7 3.7 copy-start.30
  203.5 3.0 copy-start.16
  207.0 3.6 copy-start.35
  207.9 2.7 copy-start.31
  210.6 4.0 %copy-start.39 = (bf16[2,176,2048]{2,1,0:T(8,128)(2,1)S(1)}, bf16[2,176,2048]{2,1,0:T(8,128)(2,1)}, u32[]{:S(2)}) copy-start(bf16[2,176,2048]{2,1,0:T(8,128)(2,1)} %copy-done.38) | copy-start | bytes 4325380
  214.6 4.7 %copy-start.8 = (f32[2,176,768]{2,1,0:T(8,128)S(1)}, f32[2,176,768]{2,1,0:T(8,128)}, u32[]{:S(2)}) copy-start(f32[2,176,768]{2,1,0:T(8,128)} %copy-done.7) | copy-start | bytes 3244036
  214.6 4.7 %copy-start.41 = (bf16[2,176,2048]{2,1,0:T(8,128)(2,1)S(1)}, bf16[2,176,2048]{2,1,0:T(8,128)(2,1)}, u32[]{:S(2)}) copy-start(bf16[2,176,2048]{2,1,0:T(8,128)(2,1)} %copy-done.40) | copy-start | bytes 4325380
  214.6 4.7 %copy-start.43 = (bf16[2,176,2048]{2,1,0:T(8,128)(2,1)S(1)}, bf16[2,176,2048]{2,1,0:T(8,128)(2,1)}, u32[]{:S(2)}) copy-start(bf16[2,176,2048]{2,1,0:T(8,128)(2,1)} %copy-done.42) | copy-start | bytes 4325380
  219.3 6.2 %copy-start.12 = (bf16[2,176,768]{2,1,0:T(8,128)(2,1)S(1)}, bf16[2,176,768]{2,1,0:T(8,128)(2,1)}, u32[]{:S(2)}) copy-start(bf16[2,176,768]{2,1,0:T(8,128)(2,1)} %fusion.11.normed_ref) | copy-start | bytes 1622020
  219.3 6.2 %copy-start.34 = (bf16[2,3,176,768]{3,2,1,0:T(8,128)(2,1)S(1)}, bf16[2,3,176,768]{3,2,1,0:T(8,128)(2,1)}, u32[]{:S(2)}) copy-start(bf16[2,3,176,768]{3,2,1,0:T(8,128)(2,1)} %get-tuple-element.47) | copy-start | bytes 4866052
  385.0 2.4 copy-start.11
  389.3 2.5 copy-start.10
  393.7 2.4 copy-start.1
  (14 other events, 18.2 us)

commit v2 on v1

--- a/solution.py
+++ b/solution.py
@@ -446,197 +446,220 @@
     lax.fori_loop(0, k * size, plane, 0)
 
 
+class Reduction:
+    def __init__(self, place, chunk, index, buffers, sems, out_ref, sent, parts_of):
+        self.place, self.chunk, self.out_ref, self.sent = place, chunk, out_ref, sent
+        self.held, self.core, self.near, self.last, self.far = (ref.at[index] for ref in buffers)
+        self.local = sems[0].at[index]
+        pairs = [(sems[j].at[index], sems[j + 1].at[index]) for j in range(1, len(sems), 2)]
+        self.core_sems, self.near_sems, self.last_sems = pairs[:3]
+        self.far_sems, self.flat_sems, self.pass_sems = pairs[3:]
+        self.parts_of = parts_of
+        self.loads = []
+        self.half = place.mem // 2
+
+    def begin(self):
+        for quarter in range(quarters):
+            for j, (source, first, planes) in enumerate(self.parts_of(quarter, self.place.core)):
+                copy = pltpu.make_async_copy(
+                    source, self.held.at[quarter, pl.ds(first, planes)],
+                    self.local.at[2 * quarter + j],
+                )
+                copy.start()
+                self.loads.append(copy)
+
+    def to_core(self):
+        for quarter in range(quarters):
+            parts = self.parts_of(quarter, 1 - self.place.core)
+            for j, (source, first, planes) in enumerate(parts):
+                self.sent.append(
+                    send(
+                        source, self.core.at[quarter, pl.ds(first, planes)],
+                        self.core_sems, 2 * quarter + j, self.place.other_core(),
+                    )
+                )
+
+    def from_core(self):
+        place, held, near, half = self.place, self.held, self.near, self.half
+        for copy in self.loads:
+            copy.wait()
+        for quarter in range(quarters):
+            parts = self.parts_of(quarter, place.core)
+            for j, (_, first, planes) in enumerate(parts):
+                landed = self.core.at[quarter, pl.ds(first, planes)]
+                expect(landed, self.core_sems, 2 * quarter + j, place)
+            add_planes(held, (quarter,), self.core, (quarter,), self.chunk.k, (0, place.mem))
+        for bit in range(2):
+            quarter = bit * 2 + (1 - place.near)
+            source = held.at[quarter, :, pl.ds(0, half)]
+            self.sent.append(
+                send(source, near.at[0, bit], self.near_sems, bit, place.other_quarter(1))
+            )
+            quarter = (1 - place.far) * 2 + bit
+            source = held.at[quarter, :, pl.ds(half, half)]
+            self.sent.append(
+                send(source, near.at[1, bit], self.near_sems, 2 + bit, place.other_quarter(2))
+            )
+
+    def from_near(self):
+        place, held, near, half = self.place, self.held, self.near, self.half
+        k = self.chunk.k
+        for bit in range(2):
+            expect(near.at[0, bit], self.near_sems, bit, place)
+            add_planes(held, (bit * 2 + place.near,), near, (0, bit), k, (0, half))
+            expect(near.at[1, bit], self.near_sems, 2 + bit, place)
+            add_planes(held, (place.far * 2 + bit,), near, (1, bit), k, (half, half))
+        quarter = (1 - place.far) * 2 + place.near
+        source = held.at[quarter, :, pl.ds(0, half)]
+        self.sent.append(send(source, self.last.at[0], self.last_sems, 0, place.other_quarter(2)))
+        quarter = place.far * 2 + (1 - place.near)
+        source = held.at[quarter, :, pl.ds(half, half)]
+        self.sent.append(send(source, self.last.at[1], self.last_sems, 1, place.other_quarter(1)))
+
+    def from_last(self):
+        place, half = self.place, self.half
+        for part in range(2):
+            expect(self.last.at[part], self.last_sems, part, place)
+            steps = (part * half, half)
+            add_planes(self.held, (place.quarter,), self.last, (part,), self.chunk.k, steps)
+        for step in range(1, place.mem):
+            back = place.mem - step
+            source = self.held.at[place.quarter, :, step]
+            self.sent.append(
+                send(source, self.far.at[back], self.far_sems, step, place.along(step), back)
+            )
+
+    def from_far(self):
+        place = self.place
+        for step in range(1, place.mem):
+            expect(self.far.at[step], self.far_sems, step, place)
+        k_at, rows_at = self.chunk.spot(place.quarter, place.core)
+        for k in range(self.chunk.k):
+            total = self.held[place.quarter, k, 0].astype(wide)
+            for step in range(1, place.mem):
+                total = total + self.far[step, k].astype(wide)
+            self.out_ref[k_at.start + k, rows_at, :] = total.astype(low)
+        piece = self.piece(place.quarter, place.core)
+        for turn in range(1, quarters):
+            self.sent.append(send(piece, piece, self.flat_sems, turn, place.other_quarter(turn)))
+        self.sent.append(send(piece, piece, self.pass_sems, 0, place.other_core()))
+
+    def piece(self, quarter, core):
+        k, rows = self.chunk.spot(quarter, core)
+        return self.out_ref.at[k, rows]
+
+    def from_flat(self):
+        place = self.place
+        for turn in range(1, quarters):
+            piece = self.piece(place.turn(turn), place.core)
+            expect(piece, self.flat_sems, turn, place)
+            self.sent.append(send(piece, piece, self.pass_sems, turn, place.other_core()))
+
+    def from_pass(self):
+        place = self.place
+        for turn in range(quarters):
+            piece = self.piece(place.turn(turn), 1 - place.core)
+            expect(piece, self.pass_sems, turn, place)
+
+
+def reduction_scratch(chunk, mem, model):
+    k, rows = chunk.k, chunk.rows
+
+    def room(*shape):
+        return pltpu.VMEM((2,) + shape + (rows, model), low)
+
+    buffers = [
+        room(quarters, k, mem),
+        room(quarters, k, mem),
+        room(2, 2, k, mem // 2),
+        room(2, k, mem // 2),
+        room(mem, k),
+    ]
+    sems = [pltpu.SemaphoreType.DMA((2, 2 * quarters))]
+    for count in (2 * quarters, quarters, 2, mem, quarters, quarters):
+        sems += [pltpu.SemaphoreType.DMA((2, count)) for _ in range(2)]
+    return buffers + sems
+
+
+buffer_count = 5
+reduction_refs = 18
+
+
+def start_moves(place, moves, sems, local_sems):
+    sent, stays = [], []
+    for index, (source, target) in enumerate(moves):
+        copy = pltpu.make_async_copy(source(0), target.at[place.me], local_sems.at[index])
+        copy.start()
+        stays.append(copy)
+        for step in range(1, place.mem):
+            sent.append(
+                send(
+                    source(step), target.at[place.me],
+                    (sems[0].at[index], sems[1].at[index]),
+                    step, place.along(step), place.mem - step,
+                )
+            )
+    return sent, stays
+
+
+def finish_moves(place, moves, sems, stays):
+    for index, (_, target) in enumerate(moves):
+        for step in range(1, place.mem):
+            expect(
+                target.at[(place.me + step) % place.mem],
+                (sems[0].at[index], sems[1].at[index]), step, place,
+            )
+    for copy in stays:
+        copy.wait()
+
+
 def reduce_body(
-    qkv_ref, self_out_ref, query_ref, kv_ref, cross_out_ref, in_ref, down_ref,
-    memory_ref, first_ref, second_ref, small_ref,
-    attn_out, ffn_out, memory_out, first_out, second_out, small_out,
-    held_attn, held_ffn, core_attn, core_ffn, near_attn, near_ffn, last_attn, last_ffn,
-    far_attn, far_ffn, small_far, small_flat,
-    local_sems, core_send, core_recv, near_send, near_recv, last_send, last_recv,
-    far_send, far_recv, flat_send, flat_recv, pass_send, pass_recv,
-    move_send, move_recv, small_send, small_recv,
+    qkv_ref, self_out_ref, query_ref, kv_ref, cross_out_ref,
+    memory_ref, second_ref, small_ref,
+    attn_out, memory_out, second_out, small_out,
+    small_far, small_flat, stay_sems, move_send, move_recv, small_send, small_recv,
+    *scratch,
 ):
     place = Place()
     mem = place.mem
-    half = mem // 2
-    attn_grads = [(qkv_ref, 0), (qkv_ref, 1), (qkv_ref, 2), (self_out_ref, 0)]
-    attn_grads += [(query_ref, 0), (kv_ref, 0), (kv_ref, 1), (cross_out_ref, 0)]
-    outs = (attn_out, ffn_out)
-    chunks = [Chunk(i, attn_out.shape[1], ffn_out.shape[1]) for i in range(4)]
-    helds = (held_attn, held_ffn)
-    cores = (core_attn, core_ffn)
-    nears = (near_attn, near_ffn)
-    lasts = (last_attn, last_ffn)
-    fars = (far_attn, far_ffn)
-    near_there = place.other_quarter(1)
-    far_there = place.other_quarter(2)
+    grads = [(qkv_ref, 0), (qkv_ref, 1), (qkv_ref, 2), (self_out_ref, 0)]
+    grads += [(query_ref, 0), (kv_ref, 0), (kv_ref, 1), (cross_out_ref, 0)]
     sent = []
-    loads = {}
-
-    def buffers(i):
-        kind, part = chunks[i].is_ffn, chunks[i].part
-        return tuple(group[kind].at[part] for group in (helds, cores, nears, lasts, fars))
-
-    def parts_of(i, quarter, core):
-        k, rows = chunks[i].spot(quarter, core)
-        if chunks[i].is_ffn:
-            yield in_ref.at[:, :, rows], 0, 2
-            yield down_ref.at[:, :, rows], 2, 1
-        else:
-            ref, at = attn_grads[chunks[i].part * quarters + quarter]
-            yield ref.at[pl.ds(at, 1), :, rows], 0, 1
-
-    def load(i):
-        held = buffers(i)[0]
-        for quarter in range(quarters):
-            loads[i, quarter] = []
-            for source, first, planes in parts_of(i, quarter, place.core):
-                copy = pltpu.make_async_copy(
-                    source, held.at[quarter, pl.ds(first, planes)],
-                    local_sems.at[i, quarter + first // 2 * quarters],
-                )
-                copy.start()
-                loads[i, quarter].append(copy)
-
-    def to_core(i):
-        core = buffers(i)[1]
-        for quarter in range(quarters):
-            for source, first, planes in parts_of(i, quarter, 1 - place.core):
-                sent.append(
-                    send(
-                        source, core.at[quarter, pl.ds(first, planes)],
-                        (core_send.at[i], core_recv.at[i]), quarter + first // 2 * quarters,
-                        place.other_core(),
-                    )
-                )
-
-    def from_core(i):
-        held, core, near = buffers(i)[:3]
-        for quarter in range(quarters):
-            for copy in loads[i, quarter]:
-                copy.wait()
-            sems = (core_send.at[i], core_recv.at[i])
-            if chunks[i].is_ffn:
-                expect(core.at[quarter, pl.ds(0, 2)], sems, quarter, place)
-                expect(core.at[quarter, pl.ds(2, 1)], sems, quarter + quarters, place)
-            else:
-                expect(core.at[quarter], sems, quarter, place)
-            add_planes(held, (quarter,), core, (quarter,), chunks[i].k, (0, mem))
-        sems = (near_send.at[i], near_recv.at[i])
-        for bit in range(2):
-            quarter = bit * 2 + (1 - place.near)
-            sent.append(
-                send(
-                    held.at[quarter, :, pl.ds(0, half)], near.at[0, bit], sems, bit, near_there
-                )
-            )
-            quarter = (1 - place.far) * 2 + bit
-            sent.append(
-                send(
-                    held.at[quarter, :, pl.ds(half, half)], near.at[1, bit], sems, 2 + bit, far_there
-                )
-            )
-
-    def from_near(i):
-        held, core, near, last = buffers(i)[:4]
-        sems = (near_send.at[i], near_recv.at[i])
-        for bit in range(2):
-            expect(near.at[0, bit], sems, bit, place)
-            add_planes(
-                held, (bit * 2 + place.near,), near, (0, bit), chunks[i].k, (0, half)
-            )
-            expect(near.at[1, bit], sems, 2 + bit, place)
-            add_planes(
-                held, (place.far * 2 + bit,), near, (1, bit), chunks[i].k, (half, half)
-            )
-        sems = (last_send.at[i], last_recv.at[i])
-        quarter = (1 - place.far) * 2 + place.near
-        sent.append(send(held.at[quarter, :, pl.ds(0, half)], last.at[0], sems, 0, far_there))
-        quarter = place.far * 2 + (1 - place.near)
-        sent.append(send(held.at[quarter, :, pl.ds(half, half)], last.at[1], sems, 1, near_there))
-
-    def from_last(i):
-        held, _, _, last, far = buffers(i)
-        sems = (last_send.at[i], last_recv.at[i])
-        for part in range(2):
-            expect(last.at[part], sems, part, place)
-            add_planes(
-                held, (place.quarter,), last, (part,), chunks[i].k, (part * half, half)
-            )
-        for step in range(1, mem):
-            back = mem - step
-            sent.append(
-                send(
-                    held.at[place.quarter, :, step], far.at[back],
-                    (far_send.at[i], far_recv.at[i]), step, place.along(step), back,
-                )
-            )
-
-    def from_far(i):
-        held, _, _, _, far = buffers(i)
-        for step in range(1, mem):
-            expect(far.at[step], (far_send.at[i], far_recv.at[i]), step, place)
-        kind = chunks[i].is_ffn
-        k_at, rows_at = chunks[i].spot(place.quarter, place.core)
-        for k in range(chunks[i].k):
-            total = held[place.quarter, k, 0].astype(wide)
-            for step in range(1, mem):
-                total = total + far[step, k].astype(wide)
-            outs[kind][k_at.start + k, rows_at, :] = total.astype(low)
-        piece = chunks[i].shard(outs, place.quarter, place.core)
-        for turn in range(1, quarters):
-            sent.append(
-                send(piece, piece, (flat_send.at[i], flat_recv.at[i]), turn, place.other_quarter(turn))
-            )
-        sent.append(send(piece, piece, (pass_send.at[i], pass_recv.at[i]), 0, place.other_core()))
-
-    def from_flat(i):
-        for turn in range(1, quarters):
-            piece = chunks[i].shard(outs, place.turn(turn), place.core)
-            expect(piece, (flat_send.at[i], flat_recv.at[i]), turn, place)
-            sent.append(
-                send(piece, piece, (pass_send.at[i], pass_recv.at[i]), turn, place.other_core())
-            )
-
-    def from_pass(i):
-        for turn in range(quarters):
-            piece = chunks[i].shard(outs, place.turn(turn), 1 - place.core)
-            expect(piece, (pass_send.at[i], pass_recv.at[i]), turn, place)
-
+
+    def reduction(part):
+        chunk = Chunk(part, attn_out.shape[1], 0)
+
+        def parts_of(quarter, core):
+            ref, at = grads[part * quarters + quarter]
+            return [(ref.at[pl.ds(at, 1), :, chunk.spot(quarter, core)[1]], 0, 1)]
+
+        return Reduction(
+            place, chunk, part, scratch[:buffer_count], scratch[buffer_count:], attn_out, sent,
+            parts_of,
+        )
+
+    order = [reduction(1), reduction(0)]
     moves = (
         (lambda step: memory_ref.at[:, step], memory_out),
-        (lambda step: first_ref.at[step], first_out),
         (lambda step: second_ref.at[step], second_out),
     )
-    for i in range(4):
-        load(i)
-    stays = []
-    for index, (source, target) in enumerate(moves):
-        copy = pltpu.make_async_copy(source(0), target.at[place.me], local_sems.at[4, index])
-        copy.start()
-        stays.append(copy)
+    for chunk in order:
+        chunk.begin()
     place.greet()
-    order = (2, 3, 1, 0)
-    for i in order:
-        to_core(i)
-    for index, (source, target) in enumerate(moves):
-        for step in range(1, mem):
-            sent.append(
-                send(
-                    source(step), target.at[place.me], (move_send.at[index], move_recv.at[index]),
-                    step, place.along(step), mem - step,
-                )
-            )
+    for chunk in order:
+        chunk.to_core()
     for step in range(1, mem):
         back = mem - step
         sent.append(
             send(small_ref.at[step], small_far.at[back], (small_send, small_recv), step, place.along(step), back)
         )
-    phases = (from_core, from_near, from_last, from_far, from_flat, from_pass)
+    moving, stays = start_moves(place, moves, (move_send, move_recv), stay_sems)
+    sent += moving
+    phases = ("from_core", "from_near", "from_last", "from_far", "from_flat", "from_pass")
     for time in range(len(order) + len(phases) - 1):
-        for slot, i in reversed(list(enumerate(order))):
+        for slot in reversed(range(len(order))):
             if 0 <= time - slot < len(phases):
-                phases[time - slot](i)
+                getattr(order[slot], phases[time - slot])()
         if time == 1:
             small = small_ref[0]
             for step in range(1, mem):
@@ -653,66 +676,255 @@
         expect(small_flat.at[turn], (small_send, small_recv), mem + turn, place)
         small = small + small_flat[turn]
     small_out[...] = small
-    for index, (source, target) in enumerate(moves):
-        for step in range(1, mem):
-            expect(
-                target.at[(place.me + step) % mem],
-                (move_send.at[index], move_recv.at[index]), step, place,
-            )
+    finish_moves(place, moves, (move_send, move_recv), stays)
     for copy in sent:
         copy.wait_send()
-    for copy in stays:
-        copy.wait()
-
-
-def reduce_all(attn, ffn, memory, first, second, small):
+
+
+def reduce_all(attn, memory, second, small):
     mem = lax.axis_size("mem")
     own_width, model = attn[0].shape[-2:]
-    own_hidden = ffn[0].shape[-2]
     attn_count = sum(grad.shape[0] for grad in attn)
-    ffn_count = sum(grad.shape[0] for grad in ffn)
     dma = pltpu.SemaphoreType.DMA
     in_place = pl.BlockSpec(memory_space=pl.ANY)
     held = pl.BlockSpec(memory_space=pltpu.VMEM)
-    chunks = [Chunk(i, own_width, own_hidden) for i in (0, 2)]
-
-    def both(*shape_of):
-        return [
-            pltpu.VMEM((2,) + tuple(s(c) if callable(s) else s for s in shape_of), low)
-            for c in chunks
-        ]
-
-    def k(chunk):
-        return chunk.k
-
-    def rows(chunk):
-        return chunk.rows
-
-    sem_shapes = ((4, 2 * quarters), (4, quarters), (4, 2), (4, mem), (4, quarters), (4, quarters), (3, mem), (mem + block,))
-    sems = [dma((5, 2 * quarters))]
-    for shape in sem_shapes:
-        sems += [dma(shape), dma(shape)]
     return pl.pallas_call(
         reduce_body,
-        in_specs=[in_place] * (len(attn) + len(ffn)) + [held, held, held, held],
-        out_specs=[held, held, in_place, in_place, in_place, held],
+        in_specs=[in_place] * len(attn) + [held, held, held],
+        out_specs=[held, in_place, in_place, held],
         out_shape=[
             jax.ShapeDtypeStruct((attn_count, own_width, model), low),
-            jax.ShapeDtypeStruct((ffn_count, own_hidden, model), low),
             jax.ShapeDtypeStruct((mem, memory.shape[0]) + memory.shape[2:], low),
-            jax.ShapeDtypeStruct(first.shape, low),
             jax.ShapeDtypeStruct(second.shape, low),
             jax.ShapeDtypeStruct(small.shape[1:], wide),
         ],
-        scratch_shapes=both(quarters, k, mem, rows, model)
-        + both(quarters, k, mem, rows, model)
-        + both(2, 2, k, mem // 2, rows, model)
-        + both(2, k, mem // 2, rows, model)
-        + both(mem, k, rows, model)
-        + [pltpu.VMEM((mem,) + small.shape[1:], wide), pltpu.VMEM((block,) + small.shape[1:], wide)]
-        + sems,
+        scratch_shapes=[
+            pltpu.VMEM((mem,) + small.shape[1:], wide),
+            pltpu.VMEM((block,) + small.shape[1:], wide),
+            dma((2,)), dma((2, mem)), dma((2, mem)), dma((mem + block,)), dma((mem + block,)),
+        ]
+        + reduction_scratch(Chunk(0, own_width, 0), mem, model),
         compiler_params=pltpu.CompilerParams(collective_id=1, has_side_effects=True),
-    )(*attn, *ffn, memory, first, second, small)
+    )(*attn, memory, second, small)
+
+
+def back_body(
+    in_ref, down_ref, attn_weights_ref, cross_weights_ref, self_weights_ref, sides_in, qkv_in,
+    output_ref, grad_second_ref, first_ref, input_ref, normed_one_ref, normed_two_ref,
+    self_mixed_ref, cross_mixed_ref, queries_ref, memory_ref, gain_ref,
+    ffn_out, output_out, qkv_grad_out, self_grad_out, query_grad_out, kv_grad_out,
+    cross_grad_out, memory_out, input_out, gain_out, dist_out,
+    weights_ref, cross_probs, self_probs, sides_ref, qkv_ref, mixed_grad_ref, query_grad_ref,
+    load_sems, stay_sems, move_send, move_recv, *scratch,
+):
+    place = Place()
+    sent = []
+    rows, dec_len, model = input_ref.shape
+    pairs = model // pair
+
+    def reduction(part):
+        chunk = Chunk(2 + part, 0, ffn_out.shape[1])
+
+        def parts_of(quarter, core):
+            at = chunk.spot(quarter, core)[1]
+            return [(in_ref.at[:, :, at], 0, 2), (down_ref.at[:, :, at], 2, 1)]
+
+        return Reduction(
+            place, chunk, part, scratch[:buffer_count], scratch[buffer_count:], ffn_out, sent,
+            parts_of,
+        )
+
+    one, two = reduction(0), reduction(1)
+    loads = []
+    for index, (source, target) in enumerate(
+        (
+            (attn_weights_ref.at[pl.ds(quarters, quarters)], weights_ref),
+            (sides_in, sides_ref),
+            (cross_weights_ref, cross_probs),
+            (qkv_in, qkv_ref),
+            (self_weights_ref, self_probs),
+        )
+    ):
+        copy = pltpu.make_async_copy(source, target, load_sems.at[index])
+        copy.start()
+        loads.append(copy)
+    one.begin()
+    two.begin()
+    place.greet()
+    one.to_core()
+    two.to_core()
+    moves = ((lambda step: output_ref.at[step], output_out),)
+    moving, stays = start_moves(place, moves, (move_send, move_recv), stay_sems)
+    sent += moving
+
+    def weight(k):
+        return weights_ref[k].reshape(-1, model)
+
+    def flat(values):
+        return values.reshape(-1, model)
+
+    def lanes_at(p):
+        return pl.ds(pl.multiple_of(p * pair, pair), pair)
+
+    grad_second = flat(grad_second_ref[...])
+    grad_low = grad_second.astype(low)
+    loads[0].wait()
+    mixed_grad = dot(grad_low, weight(3), 1, 1).astype(low)
+    mixed_grad_ref[...] = mixed_grad.reshape(rows, dec_len, model)
+    cross_grad_out[...] = dot(flat(cross_mixed_ref[...]), grad_low, 0, 0).astype(low)
+    one.from_core()
+    two.from_core()
+    loads[1].wait()
+    loads[2].wait()
+
+    def cross_row(r):
+        def step(p, carry):
+            at = lanes_at(p)
+            dq, dk, dv, _ = attend_back_pair(
+                [cross_probs[r, 2 * p], cross_probs[r, 2 * p + 1]],
+                queries_ref[r, :, at], sides_ref[0, r, :, at], sides_ref[1, r, :, at],
+                mixed_grad_ref[r, :, at], None,
+            )
+            query_grad_ref[r, :, at] = dq
+            sides_ref[0, r, :, at] = dk
+            sides_ref[1, r, :, at] = dv
+            return carry
+
+        lax.fori_loop(0, pairs, step, 0)
+
+    cross_row(0)
+    one.from_near()
+    for r in range(1, rows):
+        cross_row(r)
+    query_grad = flat(query_grad_ref[...])
+    query_grad_out[...] = dot(query_grad, flat(normed_two_ref[...]), 0, 0).astype(low)
+    grad_two = dot(query_grad, weight(0), 1, 0)
+    two.from_near()
+    one.from_last()
+    for k in range(2):
+        kv_grad_out[k] = dot(flat(sides_ref[k]), flat(memory_ref[...]), 0, 0).astype(low)
+
+    def encoder_row(r, carry):
+        both = dot(sides_ref[0, r], weight(1), 1, 0) + dot(sides_ref[1, r], weight(2), 1, 0)
+        memory_out[r] = both.astype(low)
+        return carry
+
+    lax.fori_loop(0, rows, encoder_row, 0)
+    two.from_last()
+    reload = pltpu.make_async_copy(
+        attn_weights_ref.at[pl.ds(0, quarters)], weights_ref, load_sems.at[5]
+    )
+    reload.start()
+
+    first = flat(first_ref[...])
+    back, gain_two = rms_back_flat(first, gain_ref[1:2, :], grad_two)
+    grad_first = grad_second + back
+    grad_low = grad_first.astype(low)
+    reload.wait()
+    mixed_grad = dot(grad_low, weight(3), 1, 1).astype(low)
+    mixed_grad_ref[...] = mixed_grad.reshape(rows, dec_len, model)
+    self_grad_out[...] = dot(flat(self_mixed_ref[...]), grad_low, 0, 0).astype(low)
+    input_out[...] = grad_first.reshape(rows, dec_len, model)
+    loads[3].wait()
+    loads[4].wait()
+
+    def self_row(r):
+        def step(p, carry):
+            at = lanes_at(p)
+            dq, dk, dv, dist = attend_back_pair(
+                [self_probs[r, 2 * p], self_probs[r, 2 * p + 1]],
+                qkv_ref[0, r, :, at], qkv_ref[1, r, :, at], qkv_ref[2, r, :, at],
+                mixed_grad_ref[r, :, at], dist_out.shape[-1],
+            )
+            qkv_ref[0, r, :, at] = dq
+            qkv_ref[1, r, :, at] = dk
+            qkv_ref[2, r, :, at] = dv
+            for half in range(2):
+                dist_out[r, 2 * p + half] = dist[half]
+            return carry
+
+        lax.fori_loop(0, pairs, step, 0)
+
+    self_row(0)
+    one.from_far()
+    for r in range(1, rows):
+        self_row(r)
+    two.from_far()
+    one.from_flat()
+
+    def project_back(k, carry):
+        grads = flat(qkv_ref[k])
+        qkv_grad_out[k] = dot(grads, flat(normed_one_ref[...]), 0, 0).astype(low)
+        return carry
+
+    lax.fori_loop(0, 3, project_back, 0)
+    grad_one = jnp.zeros((rows * dec_len, model), wide)
+    for k in range(3):
+        grad_one = grad_one + dot(flat(qkv_ref[k]), weight(k), 1, 0)
+    back, gain_one = rms_back_flat(flat(input_ref[...]).astype(wide), gain_ref[0:1, :], grad_one)
+    input_out[...] = input_out[...] + back.reshape(rows, dec_len, model)
+    gain_out[0:1, :] = gain_one
+    gain_out[1:2, :] = gain_two
+    two.from_flat()
+    one.from_pass()
+    two.from_pass()
+    finish_moves(place, moves, (move_send, move_recv), stays)
+    for copy in sent:
+        copy.wait_send()
+
+
+def back_all(
+    ffn, attn_weights, cross_weights, self_weights, sides, qkv, output,
+    grad_second, first, inputs, normed_one, normed_two, self_mixed, cross_mixed, queries,
+    memory, gains, lane_count,
+):
+    mem = lax.axis_size("mem")
+    own_hidden, model = ffn[0].shape[-2:]
+    ffn_count = sum(grad.shape[0] for grad in ffn)
+    count, heads, dec_len, _ = self_weights.shape
+    dma = pltpu.SemaphoreType.DMA
+    in_place = pl.BlockSpec(memory_space=pl.ANY)
+    held = pl.BlockSpec(memory_space=pltpu.VMEM)
+
+    def values(*shape, dtype=low):
+        return jax.ShapeDtypeStruct(shape, dtype)
+
+    return pl.pallas_call(
+        back_body,
+        in_specs=[in_place] * 7 + [held] * 11,
+        out_specs=[held, in_place] + [held] * 9,
+        out_shape=[
+            values(ffn_count, own_hidden, model),
+            values(*output.shape),
+            values(3, model, model),
+            values(model, model),
+            values(model, model),
+            values(2, model, model),
+            values(model, model),
+            values(*memory.shape),
+            values(*inputs.shape, dtype=wide),
+            values(2, model, dtype=wide),
+            values(count, heads, 1, lane_count, dtype=wide),
+        ],
+        scratch_shapes=[
+            pltpu.VMEM((quarters,) + attn_weights.shape[1:], low),
+            pltpu.VMEM(cross_weights.shape, low),
+            pltpu.VMEM(self_weights.shape, low),
+            pltpu.VMEM(sides.shape, low),
+            pltpu.VMEM(qkv.shape, low),
+            pltpu.VMEM(inputs.shape, low),
+            pltpu.VMEM(inputs.shape, low),
+            dma((6,)), dma((1,)), dma((1, mem)), dma((1, mem)),
+        ]
+        + reduction_scratch(Chunk(2, 0, own_hidden), mem, model),
+        compiler_params=pltpu.CompilerParams(
+            collective_id=2, has_side_effects=True, vmem_limit_bytes=63000000
+        ),
+    )(
+        *ffn, attn_weights, cross_weights, self_weights, sides, qkv, output,
+        grad_second, first, inputs, normed_one, normed_two, self_mixed, cross_mixed, queries,
+        memory, gains,
+    )
 
 
 def sum_blocks(values):
@@ -764,19 +976,15 @@
     return kept, mixed.astype(low)
 
 
-def attend_back_body(causal, w_ref, q_ref, k_ref, v_ref, g_ref, *rest):
-    if causal:
-        out_ref, dist_ref = rest
-    else:
-        dq_ref, dkv_ref = rest
-    queries, keys_in, values_in, grad = q_ref[0], k_ref[0], v_ref[0], g_ref[0]
-    rows, keys = queries.shape[0], keys_in.shape[0]
+def attend_back_pair(weights_pair, queries, keys_in, values_in, grad, dist_width):
+    rows, keys = weights_pair[0].shape
     dq = jnp.zeros((rows, pair), wide)
     dk = jnp.zeros((keys, pair), wide)
     dv = jnp.zeros((keys, pair), wide)
+    dist = []
     for half in range(2):
         lanes = lanes_of(half)
-        weights = w_ref[0, half]
+        weights = weights_pair[half]
         weights_wide = weights.astype(wide)
         grad_weights = dot(grad * lanes.astype(low), values_in, 1, 1)
         inner = jnp.sum(grad_weights * weights_wide, axis=-1, keepdims=True)
@@ -784,77 +992,24 @@
         dv = dv + dot(weights, grad, 0, 0) * lanes
         dq = dq + dot(grad_scores, keys_in, 1, 0) * lanes
         dk = dk + dot(grad_scores, queries, 0, 0) * lanes
-        if causal:
-            width = dist_ref.shape[-1]
+        if dist_width is not None:
             i = lax.broadcasted_iota(jnp.int32, (rows, rows), 0)
             j = lax.broadcasted_iota(jnp.int32, (rows, rows), 1)
             upside_down = dot((i + j == rows - 1).astype(wide).astype(low), grad_scores, 1, 0)
             padded = jnp.concatenate(
-                [upside_down, jnp.zeros((rows, width - keys), wide)], axis=1
+                [upside_down, jnp.zeros((rows, dist_width - keys), wide)], axis=1
             )
             turned = pltpu.roll(padded, 0, 1, stride=1, stride_axis=0)
-            dist_ref[0, 0, half : half + 1, :] = jnp.sum(turned, axis=0, keepdims=True)
-    if causal:
-        out_ref[0, 0] = dq.astype(low)
-        out_ref[0, 1] = dk.astype(low)
-        out_ref[0, 2] = dv.astype(low)
-    else:
-        dq_ref[0] = dq.astype(low)
-        dkv_ref[0, 0] = dk.astype(low)
-        dkv_ref[0, 1] = dv.astype(low)
-
-
-def column(length, k=None):
-    if k is None:
-        return pl.BlockSpec((1, length, pair), lambda r, p: (r, 0, p))
-    return pl.BlockSpec((None, 1, length, pair), lambda r, p: (k, r, 0, p))
-
-
-def cost_of(count, rows, keys, pairs, dots):
-    return pl.CostEstimate(
-        flops=count * pairs * 2 * dots * 2 * rows * keys * pair,
-        bytes_accessed=count * pairs * (2 * rows * keys * 2 + 4 * keys * pair * 2),
-        transcendentals=count * pairs * 2 * rows * keys,
-    )
-
-
-def attend_back(weights, queries, keys_in, values_in, grad, dist_width):
-    count, heads, rows, keys = weights.shape
-    pairs = heads // 2
-    width = pairs * pair
-    causal = dist_width is not None
-    if causal:
-        out_specs = [
-            pl.BlockSpec((1, 3, rows, pair), lambda r, p: (r, 0, 0, p)),
-            pl.BlockSpec((1, 1, 2, dist_width), lambda r, p: (r, p, 0, 0)),
-        ]
-        out_shape = [
-            jax.ShapeDtypeStruct((count, 3, rows, width), low),
-            jax.ShapeDtypeStruct((count, pairs, 2, dist_width), wide),
-        ]
-    else:
-        out_specs = [
-            column(rows),
-            pl.BlockSpec((1, 2, keys, pair), lambda r, p: (r, 0, 0, p)),
-        ]
-        out_shape = [
-            jax.ShapeDtypeStruct((count, rows, width), low),
-            jax.ShapeDtypeStruct((count, 2, keys, width), low),
-        ]
-    return pl.pallas_call(
-        partial(attend_back_body, causal),
-        grid=(count, pairs),
-        in_specs=[
-            pl.BlockSpec((1, 2, rows, keys), lambda r, p: (r, p, 0, 0)),
-            column(rows, queries[1]),
-            column(keys, keys_in[1]),
-            column(keys, values_in[1]),
-            column(rows),
-        ],
-        out_specs=out_specs,
-        out_shape=out_shape,
-        cost_estimate=cost_of(count, rows, keys, pairs, 4),
-    )(weights, queries[0], keys_in[0], values_in[0], grad)
+            dist.append(jnp.sum(turned, axis=0, keepdims=True))
+    return dq.astype(low), dk.astype(low), dv.astype(low), dist
+
+
+def rms_back_flat(values, gain, grad):
+    scale = lax.rsqrt(jnp.mean(values * values, axis=-1, keepdims=True) + epsilon)
+    grad_gain = jnp.sum(grad * values * scale, axis=0, keepdims=True)
+    scaled = grad * gain
+    inner = jnp.mean(scaled * values, axis=-1, keepdims=True)
+    return scaled * scale - values * (scale * scale * scale * inner), grad_gain
 
 
 def rms(values, gain):
@@ -944,23 +1099,17 @@
 
     normed_one, scale_one = rms(inputs, gain_values[0])
     (
-        attn_weights, in_weight, out_weight, memory,
+        attn_weights_in, in_weight, out_weight, memory,
         qkv, self_mixed, self_weights, first, normed_two,
         cross_queries, cross_sides, cross_mixed, cross_weights,
     ) = gather_all(
         attn_shard, ffn_shard, enc_output, padded_table,
         own_input, normed_one, gain_values, dec_ids, enc_ids, spread,
     )
-    attn_weights = attn_weights.reshape(-1, width, model)
+    cross_out_weight = attn_weights_in[7].reshape(width, model)
     in_weight = in_weight.reshape(-1, model)
     out_weight = out_weight.reshape(-1, model)
     memory = memory.reshape(count, -1, model)
-    qkv_weight = attn_weights[:3]
-    self_out_weight = attn_weights[3]
-    cross_query_weight = attn_weights[4]
-    cross_kv_weight = attn_weights[5:7]
-    cross_out_weight = attn_weights[7]
-    scale_two = rms(first, gain_values[1])[1]
     second = first + times(cross_mixed, cross_out_weight)
     normed_three, scale_three = rms(second, gain_values[2])
 
@@ -980,52 +1129,19 @@
     grad_wide = grad_out.astype(wide)
     back, gain_three = rms_back(second, scale_three, gain_values[2], grad_three)
     grad_second = grad_wide + back
-    grad_second_low = grad_second.astype(low)
-    grad_cross_mixed = times_t(grad_second_low, cross_out_weight).astype(low)
-    grad_cross_out = weight_grad(cross_mixed, grad_second_low)
-    cross_dq, cross_dkv = attend_back(
-        cross_weights,
-        (cross_queries, None),
-        (cross_sides, 0),
-        (cross_sides, 1),
-        grad_cross_mixed,
-        None,
-    )
-    grad_cross_query = weight_grad(cross_dq, normed_two)
-    grad_cross_kv = jnp.einsum(
-        "rmsc,rsd->mcd", cross_dkv, memory, preferred_element_type=wide
-    ).astype(low)
-    grad_memory = jnp.einsum(
-        "rmsc,mcd->rsd",
-        cross_dkv,
-        cross_kv_weight,
-        preferred_element_type=wide,
-    ).astype(low)
-    back, gain_two = rms_back(
-        first, scale_two, gain_values[1], times(cross_dq, cross_query_weight)
-    )
-    grad_first = grad_second + back
-    grad_first_low = grad_first.astype(low)
-    grad_self_mixed = times_t(grad_first_low, self_out_weight).astype(low)
-    grad_self_out = weight_grad(self_mixed, grad_first_low)
-    self_grads, distance_sums = attend_back(
-        self_weights, (qkv, 0), (qkv, 1), (qkv, 2), grad_self_mixed, lane_count
-    )
-    grad_qkv = jnp.einsum(
-        "rmtc,rtd->mcd", self_grads, normed_one, preferred_element_type=wide
-    ).astype(low)
+    (
+        ffn_sums, output, grad_qkv, grad_self_out, grad_cross_query, grad_cross_kv,
+        grad_cross_out, grad_memory, grad_input, gain_sums, distance_sums,
+    ) = back_all(
+        ffn_grads, attn_weights_in, cross_weights, self_weights, cross_sides, qkv,
+        jnp.stack(relative(output.astype(low), 1, mem)),
+        grad_second, first, own_input, normed_one, normed_two, self_mixed, cross_mixed,
+        cross_queries, memory, gain_values, lane_count,
+    )
     attn_grads = [
         grad.reshape(-1, mem, own_width, model)
         for grad in (grad_qkv, grad_self_out, grad_cross_query, grad_cross_kv, grad_cross_out)
     ]
-    grad_one = jnp.einsum(
-        "rmtc,mcd->rtd",
-        self_grads,
-        qkv_weight,
-        preferred_element_type=wide,
-    )
-    back, gain_one = rms_back(inputs, scale_one, gain_values[0], grad_one)
-    grad_input = grad_first + back
 
     def one_hot_of(ids):
         return (ids[:, None] == jnp.arange(bucket_count)[None, :]).astype(wide)
@@ -1040,18 +1156,16 @@
         precision=highest,
     )
     gain_grads = jnp.concatenate(
-        relative(jnp.stack([gain_one, gain_two, gain_three]), 1, mem), axis=0
+        relative(jnp.concatenate([gain_sums, gain_three[None]]), 1, mem), axis=0
     ).reshape(mem, 3 * own_width)
     small = jnp.concatenate(
         [gain_grads, grad_table.reshape(mem, own_heads * bucket_count)], axis=1
     )
     small_size = small.shape[1]
     small = jnp.pad(small, ((0, 0), (0, 8 * pair - small_size))).reshape(mem, 8, pair)
-    attn_sums, ffn_sums, grad_memory, output, grad_input, small = reduce_all(
+    attn_sums, grad_memory, grad_input, small = reduce_all(
         attn_grads,
-        ffn_grads,
         grad_memory.reshape(count, mem, enc_len // mem, model),
-        jnp.stack(relative(output.astype(low), 1, mem)),
         jnp.stack(relative(grad_input.astype(low), 1, mem)),
         small,
     )

time: 401 us -> 367 us (0.915)
  matrix products: 49.7 us -> 23.1 us
  local copies, waits for them, and re-layouts: 40 us -> 27.5 us
    dot_general x4 -> x0, matrix products: 18 us -> none  [the longest x1 6.48 us: shards(): jnp.einsum('rmsc,mcd->rsd', cross_dkv, cross_kv_weight, preferred_element...]
    slice x4 -> x2, local copies, waits for them, and re-layouts: 11.2 us -> 1.49 us  [the longest x1 1.47 us: shards(): cross_out_weight = attn_weights_in[7].reshape(width, model)]
    dot_general x5 -> x2, matrix products: 16.4 us -> 9.38 us  [weight_grad(): jnp.einsum('rtc,rtd->cd', grads, values, preferred_element_type=wide)]
    pallas_call x3 -> x2, Pallas kernels: 177 us -> 180 us  [the longest x1 90.2 us: back_all(): pl.pallas_call(back_body, in_specs=[in_place] * 7 + [held] * 11, out_spec...]
    unnamed x110 -> x62, local copies, waits for them, and re-layouts: 15.4 us -> 12.8 us
    dot_general x4 -> x2, matrix products: 8.84 us -> 8.95 us  [times_t(): jnp.einsum('rtd,cd->rtc', values, weight, preferred_element_type=wide)]
where the time goes in v2:
time: 367 us; the launch traced here: 363 us
  Pallas kernels  294 us (80%)
  local copies, waits for them, and re-layouts  27.5 us (7%)
  matrix products  23.1 us (6%)
  other arithmetic  17.5 us (5%)
    pallas_call x1, Pallas kernels, gather_all(): pl.pallas_call(gather_body, in_specs=[held, held, in_place] + [held] * (l...  114 us
    pallas_call x1, Pallas kernels, back_all(): pl.pallas_call(back_body, in_specs=[in_place] * 7 + [held] * 11, out_spec...  90.2 us
    pallas_call x1, Pallas kernels, reduce_all(): pl.pallas_call(reduce_body, in_specs=[in_place] * len(attn) + [held, held...  89.7 us
    unnamed x62, local copies, waits for them, and re-layouts  12.8 us
    dot_general x2, matrix products, weight_grad(): jnp.einsum('rtc,rtd->cd', grads, values, preferred_element_type=wide)  9.38 us
    dot_general x2, matrix products, times_t(): jnp.einsum('rtd,cd->rtc', values, weight, preferred_element_type=wide)  8.95 us

profile of v2, /device:TPU:25, one launch (start us, length us, event | category | flops | bytes accessed | tf_op | source)
XLA Modules:
  0.0 363.4 jit_solution(8639190105056743937)
XLA Ops:
  0.8 1.2 slice.80
  4.5 0.9 fusion.30
  9.2 0.8 copy.38.dec_column_ref
  10.1 1.3 fusion.9
  11.4 1.0 fusion.11.normed_ref.normed_one_ref
  13.2 2.9 pad_maximum_fusion.1.ffn_ref
  17.3 1.4 copy-done.4
  18.7 114.0 %shard_map.255 = (bf16[8,4,192,768]{3,2,1,0:T(8,128)(2,1)}, bf16[2,4,512,768]{3,2,1,0:T(8,128)(2,1)}, bf16[1,4,512,768]{3,2,1,0:T(8,128)(2,1)}, bf16[2,4,128,768...) custom-call(bf16[8,192,768]{2,1,0:T(8,128)(2,1)} %copy-done.4, ...), custom_call_target="tpu_custom_call" | custom-call | tf_op jit(solution)/shard_map/pallas_call | solution.py:398
  132.7 1.5 slice.82
  135.2 5.4 %fusion.15 = f32[2,176,4096]{2,1,0:T(8,128)S(1)} fusion(bf16[4096,768,1]{1,0,2:T(8,128)(2,1)} %bitcast.153, f32[2,176,768]{2,1,0:T(8,128)S(1)} %get-tuple-element.129, f32[768]{0:T(1024)S(1)} %get-tuple-element.97, f32[2,176]{1,0:T(2,128)S(1)} %add_rsqrt_fusion), kind=kOutput, calls=%fused_computation.62 | convolution fusion | flops 2215403520 | bytes 13144448 | tf_op jit(solution)/shard_map/rtd,cd->rtc/dot_general | solution.py:1028
  140.6 3.6 fusion.6
  144.2 1.3 fusion.8
  145.5 2.6 multiply_reduce_fusion
  148.1 1.3 subtract_add_fusion.grad_second_ref
  149.5 0.9 pad_maximum_fusion.4.output_ref
  150.4 3.5 bitcast_convert_fusion.1
  153.9 5.9 %bitcast_convert_fusion = bf16[4096,768]{1,0:T(8,128)(2,1)} fusion(bf16[2,176,2048]{2,1,0:T(8,128)(2,1)S(1)} %get-tuple-element.102, bf16[2,176,2048]{2,1,0:T(8,128)(2,1)S(1)} %get-tuple-element.101, f32[2,176,768]{2,1,0:T(8,128)S(1)} %get-tuple-element.129, f32[768]{0:T(1024)S(1)} %get-tuple-element.97, f32[2,176]{1,0:T(2,128)S(1)} %add_rsqrt_fusion), kind=kOutput, calls=%fused_computation | convolution fusion | flops 2224316416 | bytes 10260864 | tf_op jit(solution)/shard_map/rtc,rtd->cd/dot_general | solution.py:1036
  159.8 90.2 %shard_map.256 = (bf16[3,512,768]{2,1,0:T(8,128)(2,1)}, bf16[4,2,44,768]{3,2,1,0:T(8,128)(2,1)}, bf16[3,768,768]{2,1,0:T(8,128)(2,1)}, bf16[768,768]{1,0:T(8,128...) custom-call(bf16[2,4,512,768]{3,2,1,0:T(8,128)(2,1)} %bitcast.136, ...), custom_call_target="tpu_custom_call" | custom-call | tf_op jit(solution)/shard_map/pallas_call | solution.py:892
  250.0 0.9 fusion.23
  252.7 1.3 convert_element_type.82
  254.2 0.9 pad_maximum_fusion.5.second_ref
  255.1 89.7 %shard_map.257 = (bf16[8,192,768]{2,1,0:T(8,128)(2,1)}, bf16[4,2,128,768]{3,2,1,0:T(8,128)(2,1)}, bf16[4,2,44,768]{3,2,1,0:T(8,128)(2,1)}, f32[8,128]{1,0:T(8,128)}) custom-call(bf16[3,4,192,768]{3,2,1,0:T(8,128)(2,1)} %bitcast.138, bf16[1,4,192,768]{3,2,1,0:T(8,128)(2,1)} %bitcast.145, bf16[1,4,192,768]{3,2,1,0:T(8,128)(2,1)} %bitcast.146, ...), custom_call_target="tpu_custom_call" | custom-call | tf_op jit(solution)/shard_map/pallas_call | solution.py:691
  344.8 1.4 reshape.136
  347.6 1.2 bitcast_convert_fusion.3
  348.7 1.6 copy.40
  350.5 1.6 copy.39
  352.1 2.0 bitcast_convert_fusion.2
  355.0 1.4 slice_bitcast_fusion.4
  356.4 1.6 slice_bitcast_fusion.2
  358.0 1.0 copy-done.5
  359.3 1.2 slice_bitcast_fusion.1
  360.8 2.4 copy.41
  (92 shorter events, 14.3 us)
Async XLA Ops:
  0.6 5.3 %copy-start = (s32[8,176]{1,0:T(8,128)S(1)}, s32[8,176]{1,0:T(8,128)}, u32[]{:S(2)}) copy-start(s32[8,176]{1,0:T(8,128)} %param.18) | copy-start | bytes 16900
  8.6 3.9 %copy-start.17 = (f32[3,768]{1,0:T(4,128)}, f32[3,768]{1,0:T(4,128)S(1)}, u32[]{:S(2)}) copy-start(f32[3,768]{1,0:T(4,128)S(1)} %convert_element_type.69.gain_ref) | copy-start | bytes 27652
  10.1 2.4 copy-start.8
  11.4 1.4 copy-start.2
  13.1 2.9 copy-start.13
  13.1 3.0 copy-start.11
  13.1 3.0 copy-start.14
  16.0 1.0 copy-start.15
  16.0 1.2 copy-start.12
  16.0 1.2 copy-start.16
  17.3 1.4 copy-start.4
  132.7 1.6 copy-start.3
  132.7 1.7 copy-start.7
  135.1 5.4 %copy-start.18 = (bf16[8,176,768]{2,1,0:T(8,128)(2,1)S(1)}, bf16[8,176,768]{2,1,0:T(8,128)(2,1)}, u32[]{:S(2)}) copy-start(bf16[8,176,768]{2,1,0:T(8,128)(2,1)} %param.31) | copy-start | bytes 6488068
  135.1 5.4 %copy-start.19 = (bf16[1,4,512,768]{3,2,1,0:T(8,128)(2,1)S(1)}, bf16[1,4,512,768]{3,2,1,0:T(8,128)(2,1)}, u32[]{:S(2)}) copy-start(bf16[1,4,512,768]{3,2,1,0:T(8,128)(2,1)} %get-tuple-element.41) | copy-start | bytes 9437188
  135.2 10.3 %slice-start = ((s8[6291456]{0:T(1024)(128)(4,1)}), s8[4194304]{0:T(1024)(128)(4,1)S(1)}, s32[]{:S(2)}) async-start(s8[6291456]{0:T(1024)(128)(4,1)} %bitcast.154), calls=%async_computation | async-start | bytes 8388608
  140.6 4.9 %slice-start.1 = ((s8[6291456]{0:T(1024)(128)(4,1)}), s8[2097152]{0:T(1024)(128)(4,1)S(1)}, s32[]{:S(2)}) async-start(s8[6291456]{0:T(1024)(128)(4,1)} %bitcast.154), calls=%async_computation.1 | async-start | bytes 4194304
  344.8 5.5 %copy-start.10 = (bf16[4,2,44,768]{3,2,1,0:T(8,128)(2,1)S(1)}, bf16[4,2,44,768]{3,2,1,0:T(8,128)(2,1)}, u32[]{:S(2)}) copy-start(bf16[4,2,44,768]{3,2,1,0:T(8,128)(2,1)} %get-tuple-element.54) | copy-start | bytes 1622020
  350.3 1.8 copy-start.9
  352.1 2.4 copy-start.6
  356.4 2.5 copy-start.5
  360.6 2.6 copy-start.1

commit v3 on v2

--- a/solution.py
+++ b/solution.py
@@ -447,11 +447,12 @@
 
 
 class Reduction:
-    def __init__(self, place, chunk, index, buffers, sems, out_ref, sent, parts_of):
+    def __init__(self, place, chunk, held, index, scratch, out_ref, sent, parts_of):
         self.place, self.chunk, self.out_ref, self.sent = place, chunk, out_ref, sent
-        self.held, self.core, self.near, self.last, self.far = (ref.at[index] for ref in buffers)
-        self.local = sems[0].at[index]
-        pairs = [(sems[j].at[index], sems[j + 1].at[index]) for j in range(1, len(sems), 2)]
+        self.held = held
+        refs = [ref.at[index] for ref in scratch]
+        self.core, self.near, self.last, self.far, self.local = refs[:5]
+        pairs = [(refs[j], refs[j + 1]) for j in range(5, len(refs), 2)]
         self.core_sems, self.near_sems, self.last_sems = pairs[:3]
         self.far_sems, self.flat_sems, self.pass_sems = pairs[3:]
         self.parts_of = parts_of
@@ -570,7 +571,6 @@
 
     buffers = [
         room(quarters, k, mem),
-        room(quarters, k, mem),
         room(2, 2, k, mem // 2),
         room(2, k, mem // 2),
         room(mem, k),
@@ -581,148 +581,51 @@
     return buffers + sems
 
 
-buffer_count = 5
-reduction_refs = 18
-
-
-def start_moves(place, moves, sems, local_sems):
-    sent, stays = [], []
-    for index, (source, target) in enumerate(moves):
-        copy = pltpu.make_async_copy(source(0), target.at[place.me], local_sems.at[index])
-        copy.start()
-        stays.append(copy)
+reduction_refs = 17
+
+
+class Move:
+    def __init__(self, place, index, source, target, sems):
+        self.place, self.target = place, target
+        self.sems = (sems[0].at[index], sems[1].at[index])
+        self.stay = pltpu.make_async_copy(source(0), target(place.me), sems[2].at[index])
+        self.stay.start()
+        self.sent = [
+            send(
+                source(step), target(place.me), self.sems, step, place.along(step),
+                place.mem - step,
+            )
+            for step in range(1, place.mem)
+        ]
+
+    def finish(self):
+        place = self.place
         for step in range(1, place.mem):
-            sent.append(
-                send(
-                    source(step), target.at[place.me],
-                    (sems[0].at[index], sems[1].at[index]),
-                    step, place.along(step), place.mem - step,
-                )
-            )
-    return sent, stays
-
-
-def finish_moves(place, moves, sems, stays):
-    for index, (_, target) in enumerate(moves):
-        for step in range(1, place.mem):
-            expect(
-                target.at[(place.me + step) % place.mem],
-                (sems[0].at[index], sems[1].at[index]), step, place,
-            )
-    for copy in stays:
-        copy.wait()
-
-
-def reduce_body(
-    qkv_ref, self_out_ref, query_ref, kv_ref, cross_out_ref,
-    memory_ref, second_ref, small_ref,
-    attn_out, memory_out, second_out, small_out,
-    small_far, small_flat, stay_sems, move_send, move_recv, small_send, small_recv,
-    *scratch,
+            expect(self.target((place.me + step) % place.mem), self.sems, step, place)
+        for copy in self.sent:
+            copy.wait_send()
+        self.stay.wait()
+
+
+def back_body(
+    in_ref, down_ref, attn_weights_ref, cross_weights_ref, self_weights_ref, sides_in, qkv_in,
+    output_ref, grad_second_ref, first_ref, input_ref, normed_one_ref, normed_two_ref,
+    self_mixed_ref, cross_mixed_ref, queries_ref, memory_ref, gain_ref, gain_three_ref,
+    attn_out, ffn_out, output_out, memory_out, input_out, small_out,
+    held_ffn, grads_ref, weights_ref, cross_probs, self_probs, sides_ref, qkv_ref,
+    mixed_grad_ref, query_grad_ref, grad_first_ref, memory_blocks, input_blocks,
+    small_ref, small_far, small_flat,
+    load_sems, move_send, move_recv, stay_sems, small_send, small_recv, *scratch,
 ):
     place = Place()
     mem = place.mem
-    grads = [(qkv_ref, 0), (qkv_ref, 1), (qkv_ref, 2), (self_out_ref, 0)]
-    grads += [(query_ref, 0), (kv_ref, 0), (kv_ref, 1), (cross_out_ref, 0)]
-    sent = []
-
-    def reduction(part):
-        chunk = Chunk(part, attn_out.shape[1], 0)
-
-        def parts_of(quarter, core):
-            ref, at = grads[part * quarters + quarter]
-            return [(ref.at[pl.ds(at, 1), :, chunk.spot(quarter, core)[1]], 0, 1)]
-
-        return Reduction(
-            place, chunk, part, scratch[:buffer_count], scratch[buffer_count:], attn_out, sent,
-            parts_of,
-        )
-
-    order = [reduction(1), reduction(0)]
-    moves = (
-        (lambda step: memory_ref.at[:, step], memory_out),
-        (lambda step: second_ref.at[step], second_out),
-    )
-    for chunk in order:
-        chunk.begin()
-    place.greet()
-    for chunk in order:
-        chunk.to_core()
-    for step in range(1, mem):
-        back = mem - step
-        sent.append(
-            send(small_ref.at[step], small_far.at[back], (small_send, small_recv), step, place.along(step), back)
-        )
-    moving, stays = start_moves(place, moves, (move_send, move_recv), stay_sems)
-    sent += moving
-    phases = ("from_core", "from_near", "from_last", "from_far", "from_flat", "from_pass")
-    for time in range(len(order) + len(phases) - 1):
-        for slot in reversed(range(len(order))):
-            if 0 <= time - slot < len(phases):
-                getattr(order[slot], phases[time - slot])()
-        if time == 1:
-            small = small_ref[0]
-            for step in range(1, mem):
-                expect(small_far.at[step], (small_send, small_recv), step, place)
-                small = small + small_far[step]
-            small_flat[0] = small
-            for turn in range(1, block):
-                there = place.at(place.turn(turn // 2), (place.core + turn % 2) % 2)
-                sent.append(
-                    send(small_flat.at[0], small_flat.at[turn], (small_send, small_recv), mem + turn, there)
-                )
-    small = small_flat[0]
-    for turn in range(1, block):
-        expect(small_flat.at[turn], (small_send, small_recv), mem + turn, place)
-        small = small + small_flat[turn]
-    small_out[...] = small
-    finish_moves(place, moves, (move_send, move_recv), stays)
-    for copy in sent:
-        copy.wait_send()
-
-
-def reduce_all(attn, memory, second, small):
-    mem = lax.axis_size("mem")
-    own_width, model = attn[0].shape[-2:]
-    attn_count = sum(grad.shape[0] for grad in attn)
-    dma = pltpu.SemaphoreType.DMA
-    in_place = pl.BlockSpec(memory_space=pl.ANY)
-    held = pl.BlockSpec(memory_space=pltpu.VMEM)
-    return pl.pallas_call(
-        reduce_body,
-        in_specs=[in_place] * len(attn) + [held, held, held],
-        out_specs=[held, in_place, in_place, held],
-        out_shape=[
-            jax.ShapeDtypeStruct((attn_count, own_width, model), low),
-            jax.ShapeDtypeStruct((mem, memory.shape[0]) + memory.shape[2:], low),
-            jax.ShapeDtypeStruct(second.shape, low),
-            jax.ShapeDtypeStruct(small.shape[1:], wide),
-        ],
-        scratch_shapes=[
-            pltpu.VMEM((mem,) + small.shape[1:], wide),
-            pltpu.VMEM((block,) + small.shape[1:], wide),
-            dma((2,)), dma((2, mem)), dma((2, mem)), dma((mem + block,)), dma((mem + block,)),
-        ]
-        + reduction_scratch(Chunk(0, own_width, 0), mem, model),
-        compiler_params=pltpu.CompilerParams(collective_id=1, has_side_effects=True),
-    )(*attn, memory, second, small)
-
-
-def back_body(
-    in_ref, down_ref, attn_weights_ref, cross_weights_ref, self_weights_ref, sides_in, qkv_in,
-    output_ref, grad_second_ref, first_ref, input_ref, normed_one_ref, normed_two_ref,
-    self_mixed_ref, cross_mixed_ref, queries_ref, memory_ref, gain_ref,
-    ffn_out, output_out, qkv_grad_out, self_grad_out, query_grad_out, kv_grad_out,
-    cross_grad_out, memory_out, input_out, gain_out, dist_out,
-    weights_ref, cross_probs, self_probs, sides_ref, qkv_ref, mixed_grad_ref, query_grad_ref,
-    load_sems, stay_sems, move_send, move_recv, *scratch,
-):
-    place = Place()
     sent = []
     rows, dec_len, model = input_ref.shape
     pairs = model // pair
-
-    def reduction(part):
+    heads = 2 * pairs
+    own_heads = heads // mem
+
+    def ffn_reduction(part):
         chunk = Chunk(2 + part, 0, ffn_out.shape[1])
 
         def parts_of(quarter, core):
@@ -730,35 +633,53 @@
             return [(in_ref.at[:, :, at], 0, 2), (down_ref.at[:, :, at], 2, 1)]
 
         return Reduction(
-            place, chunk, part, scratch[:buffer_count], scratch[buffer_count:], ffn_out, sent,
+            place, chunk, held_ffn.at[part], part, scratch[:reduction_refs], ffn_out, sent,
             parts_of,
         )
 
-    one, two = reduction(0), reduction(1)
-    loads = []
-    for index, (source, target) in enumerate(
-        (
-            (attn_weights_ref.at[pl.ds(quarters, quarters)], weights_ref),
-            (sides_in, sides_ref),
-            (cross_weights_ref, cross_probs),
-            (qkv_in, qkv_ref),
-            (self_weights_ref, self_probs),
+    def attn_reduction(part):
+        chunk = Chunk(part, attn_out.shape[1], 0)
+
+        def parts_of(quarter, core):
+            return [(grads_ref.at[part * quarters + quarter, :, :, core], 0, 1)]
+
+        held = grads_ref.at[pl.ds(part * quarters, quarters), :, :, place.core]
+        return Reduction(
+            place, chunk, held, part, scratch[reduction_refs:], attn_out, sent, parts_of
         )
-    ):
+
+    one, two = ffn_reduction(0), ffn_reduction(1)
+    third, fourth = attn_reduction(1), attn_reduction(0)
+
+    def load(index, source, target):
         copy = pltpu.make_async_copy(source, target, load_sems.at[index])
         copy.start()
-        loads.append(copy)
+        return copy
+
+    def load_weight(index, k, slot):
+        return load(index, attn_weights_ref.at[k], weights_ref.at[slot])
+
+    got_out = load_weight(0, 7, 0)
+    got_sides = load(1, sides_in, sides_ref)
+    got_probs = load(2, cross_weights_ref.at[0], cross_probs)
+    got_kv = [load_weight(3, 5, 1), load_weight(4, 6, 2)]
     one.begin()
     two.begin()
+    got_qkv = load(5, qkv_in, qkv_ref)
+    got_self_probs = load(6, self_weights_ref.at[0], self_probs)
     place.greet()
     one.to_core()
     two.to_core()
-    moves = ((lambda step: output_ref.at[step], output_out),)
-    moving, stays = start_moves(place, moves, (move_send, move_recv), stay_sems)
-    sent += moving
-
-    def weight(k):
-        return weights_ref[k].reshape(-1, model)
+    moves = []
+
+    def move(source, target):
+        sems = (move_send, move_recv, stay_sems)
+        moves.append(Move(place, len(moves), source, target, sems))
+
+    move(lambda step: output_ref.at[step], lambda d: output_out.at[d])
+
+    def weight(slot):
+        return weights_ref[slot].reshape(-1, model)
 
     def flat(values):
         return values.reshape(-1, model)
@@ -766,22 +687,27 @@
     def lanes_at(p):
         return pl.ds(pl.multiple_of(p * pair, pair), pair)
 
-    grad_second = flat(grad_second_ref[...])
-    grad_low = grad_second.astype(low)
-    loads[0].wait()
-    mixed_grad = dot(grad_low, weight(3), 1, 1).astype(low)
+    def keep(k, grad):
+        grads_ref[k] = grad.astype(low).reshape(grads_ref.shape[1:])
+
+    grad_low = flat(grad_second_ref[...]).astype(low)
+    got_out.wait()
+    mixed_grad = dot(grad_low, weight(0), 1, 1).astype(low)
     mixed_grad_ref[...] = mixed_grad.reshape(rows, dec_len, model)
-    cross_grad_out[...] = dot(flat(cross_mixed_ref[...]), grad_low, 0, 0).astype(low)
+    got_query = load_weight(7, 4, 0)
     one.from_core()
+    keep(7, dot(flat(cross_mixed_ref[...]), grad_low, 0, 0))
     two.from_core()
-    loads[1].wait()
-    loads[2].wait()
+    got_sides.wait()
+    got_probs.wait()
+    for copy in got_kv:
+        copy.wait()
 
     def cross_row(r):
         def step(p, carry):
             at = lanes_at(p)
             dq, dk, dv, _ = attend_back_pair(
-                [cross_probs[r, 2 * p], cross_probs[r, 2 * p + 1]],
+                [cross_probs[2 * p], cross_probs[2 * p + 1]],
                 queries_ref[r, :, at], sides_ref[0, r, :, at], sides_ref[1, r, :, at],
                 mixed_grad_ref[r, :, at], None,
             )
@@ -791,84 +717,140 @@
             return carry
 
         lax.fori_loop(0, pairs, step, 0)
+        if r + 1 < rows:
+            following = load(8 + r, cross_weights_ref.at[r + 1], cross_probs)
+        both = dot(sides_ref[0, r], weight(1), 1, 0) + dot(sides_ref[1, r], weight(2), 1, 0)
+        memory_blocks[r] = both.astype(low).reshape(memory_blocks.shape[1:])
+        if r + 1 < rows:
+            following.wait()
+
+    def move_memory(r):
+        move(lambda step: memory_blocks.at[r, step], lambda d: memory_out.at[d, r])
 
     cross_row(0)
+    move_memory(0)
     one.from_near()
     for r in range(1, rows):
         cross_row(r)
+    got_self_out = load_weight(3, 3, 1)
     query_grad = flat(query_grad_ref[...])
-    query_grad_out[...] = dot(query_grad, flat(normed_two_ref[...]), 0, 0).astype(low)
+    keep(4, dot(query_grad, flat(normed_two_ref[...]), 0, 0))
+    two.from_near()
+    for k in range(2):
+        keep(5 + k, dot(flat(sides_ref[k]), flat(memory_ref[...]), 0, 0))
+    third.to_core()
+    one.from_last()
+
+    got_query.wait()
     grad_two = dot(query_grad, weight(0), 1, 0)
-    two.from_near()
-    one.from_last()
-    for k in range(2):
-        kv_grad_out[k] = dot(flat(sides_ref[k]), flat(memory_ref[...]), 0, 0).astype(low)
-
-    def encoder_row(r, carry):
-        both = dot(sides_ref[0, r], weight(1), 1, 0) + dot(sides_ref[1, r], weight(2), 1, 0)
-        memory_out[r] = both.astype(low)
-        return carry
-
-    lax.fori_loop(0, rows, encoder_row, 0)
+    back, gain_two = rms_back_flat(flat(first_ref[...]), gain_ref[1:2, :], grad_two)
+    grad_first = flat(grad_second_ref[...]) + back
+    grad_first_ref[...] = grad_first
+    grad_low = grad_first.astype(low)
+    got_self_out.wait()
+    mixed_grad = dot(grad_low, weight(1), 1, 1).astype(low)
+    mixed_grad_ref[...] = mixed_grad.reshape(rows, dec_len, model)
+    got_qkv_weights = [load_weight(7, 0, 0), load_weight(3, 1, 1), load_weight(4, 2, 2)]
+    third.from_core()
     two.from_last()
-    reload = pltpu.make_async_copy(
-        attn_weights_ref.at[pl.ds(0, quarters)], weights_ref, load_sems.at[5]
-    )
-    reload.start()
-
-    first = flat(first_ref[...])
-    back, gain_two = rms_back_flat(first, gain_ref[1:2, :], grad_two)
-    grad_first = grad_second + back
-    grad_low = grad_first.astype(low)
-    reload.wait()
-    mixed_grad = dot(grad_low, weight(3), 1, 1).astype(low)
-    mixed_grad_ref[...] = mixed_grad.reshape(rows, dec_len, model)
-    self_grad_out[...] = dot(flat(self_mixed_ref[...]), grad_low, 0, 0).astype(low)
-    input_out[...] = grad_first.reshape(rows, dec_len, model)
-    loads[3].wait()
-    loads[4].wait()
+    for r in range(1, rows):
+        move_memory(r)
+    keep(3, dot(flat(self_mixed_ref[...]), grad_low, 0, 0))
+    got_qkv.wait()
+    got_self_probs.wait()
 
     def self_row(r):
         def step(p, carry):
             at = lanes_at(p)
             dq, dk, dv, dist = attend_back_pair(
-                [self_probs[r, 2 * p], self_probs[r, 2 * p + 1]],
+                [self_probs[2 * p], self_probs[2 * p + 1]],
                 qkv_ref[0, r, :, at], qkv_ref[1, r, :, at], qkv_ref[2, r, :, at],
-                mixed_grad_ref[r, :, at], dist_out.shape[-1],
+                mixed_grad_ref[r, :, at], small_ref.shape[-1],
             )
             qkv_ref[0, r, :, at] = dq
             qkv_ref[1, r, :, at] = dk
             qkv_ref[2, r, :, at] = dv
             for half in range(2):
-                dist_out[r, 2 * p + half] = dist[half]
+                spot = 2 * p + half
+                owner = (place.me + lax.div(spot, own_heads)) % mem
+                head = owner * own_heads + lax.rem(spot, own_heads)
+                small_ref[head] = dist[half] if r == 0 else small_ref[head] + dist[half]
             return carry
 
         lax.fori_loop(0, pairs, step, 0)
+        if r + 1 < rows:
+            following = load(8 + r, self_weights_ref.at[r + 1], self_probs)
+            following.wait()
 
     self_row(0)
+    third.from_near()
     one.from_far()
     for r in range(1, rows):
         self_row(r)
+    third.from_last()
     two.from_far()
     one.from_flat()
 
     def project_back(k, carry):
-        grads = flat(qkv_ref[k])
-        qkv_grad_out[k] = dot(grads, flat(normed_one_ref[...]), 0, 0).astype(low)
+        keep(k, dot(flat(qkv_ref[k]), flat(normed_one_ref[...]), 0, 0))
         return carry
 
     lax.fori_loop(0, 3, project_back, 0)
-    grad_one = jnp.zeros((rows * dec_len, model), wide)
-    for k in range(3):
+    fourth.to_core()
+    for copy in got_qkv_weights:
+        copy.wait()
+    grad_one = dot(flat(qkv_ref[0]), weight(0), 1, 0)
+    fourth.from_core()
+    for k in range(1, 3):
         grad_one = grad_one + dot(flat(qkv_ref[k]), weight(k), 1, 0)
     back, gain_one = rms_back_flat(flat(input_ref[...]).astype(wide), gain_ref[0:1, :], grad_one)
-    input_out[...] = input_out[...] + back.reshape(rows, dec_len, model)
-    gain_out[0:1, :] = gain_one
-    gain_out[1:2, :] = gain_two
+    grad_input = (grad_first_ref[...] + back).astype(low).reshape(rows, dec_len, model)
+    own_len = dec_len // mem
+    for d in range(mem):
+        input_blocks[d] = grad_input[:, d * own_len : (d + 1) * own_len, :]
+    size = small_ref.shape[-1]
+    for index, gain_grad in enumerate((gain_one, gain_two, gain_three_ref[...])):
+        for j in range(model // size):
+            spot = heads + index * (model // size) + j
+            small_ref[spot] = gain_grad[:, j * size : (j + 1) * size]
+    for step in range(1, mem):
+        back_step = mem - step
+        sent.append(
+            send(
+                small_ref, small_far.at[back_step], (small_send, small_recv), step,
+                place.along(step), back_step,
+            )
+        )
     two.from_flat()
     one.from_pass()
+    third.from_far()
+    fourth.from_near()
+    move(
+        lambda step: input_blocks.at[(place.me + step) % mem], lambda d: input_out.at[d]
+    )
+    total = small_ref[...]
+    for step in range(1, mem):
+        expect(small_far.at[step], (small_send, small_recv), step, place)
+        total = total + small_far[step]
+    small_flat[0] = total
+    for turn in range(1, block):
+        there = place.at(place.turn(turn // 2), (place.core + turn % 2) % 2)
+        sems = (small_send, small_recv)
+        sent.append(send(small_flat.at[0], small_flat.at[turn], sems, mem + turn, there))
     two.from_pass()
-    finish_moves(place, moves, (move_send, move_recv), stays)
+    third.from_flat()
+    fourth.from_last()
+    third.from_pass()
+    total = small_flat[0]
+    for turn in range(1, block):
+        expect(small_flat.at[turn], (small_send, small_recv), mem + turn, place)
+        total = total + small_flat[turn]
+    small_out[...] = total
+    fourth.from_far()
+    fourth.from_flat()
+    fourth.from_pass()
+    for moving in moves:
+        moving.finish()
     for copy in sent:
         copy.wait_send()
 
@@ -876,54 +858,64 @@
 def back_all(
     ffn, attn_weights, cross_weights, self_weights, sides, qkv, output,
     grad_second, first, inputs, normed_one, normed_two, self_mixed, cross_mixed, queries,
-    memory, gains, lane_count,
+    memory, gains, gain_three, lane_count,
 ):
     mem = lax.axis_size("mem")
     own_hidden, model = ffn[0].shape[-2:]
-    ffn_count = sum(grad.shape[0] for grad in ffn)
+    own_width = attn_weights.shape[2]
     count, heads, dec_len, _ = self_weights.shape
+    enc_len = memory.shape[1]
+    small_shape = (heads + 3 * (model // lane_count), 1, lane_count)
     dma = pltpu.SemaphoreType.DMA
     in_place = pl.BlockSpec(memory_space=pl.ANY)
     held = pl.BlockSpec(memory_space=pltpu.VMEM)
+    attn_chunk, ffn_chunk = Chunk(0, own_width, 0), Chunk(2, 0, own_hidden)
+    move_count = count + 2
 
     def values(*shape, dtype=low):
         return jax.ShapeDtypeStruct(shape, dtype)
 
     return pl.pallas_call(
         back_body,
-        in_specs=[in_place] * 7 + [held] * 11,
-        out_specs=[held, in_place] + [held] * 9,
+        in_specs=[in_place] * 7 + [held] * 12,
+        out_specs=[held, held, in_place, in_place, in_place, held],
         out_shape=[
-            values(ffn_count, own_hidden, model),
+            values(2 * quarters, own_width, model),
+            values(3, own_hidden, model),
             values(*output.shape),
-            values(3, model, model),
-            values(model, model),
-            values(model, model),
-            values(2, model, model),
-            values(model, model),
-            values(*memory.shape),
-            values(*inputs.shape, dtype=wide),
-            values(2, model, dtype=wide),
-            values(count, heads, 1, lane_count, dtype=wide),
+            values(mem, count, enc_len // mem, model),
+            values(*output.shape),
+            values(*small_shape, dtype=wide),
         ],
         scratch_shapes=[
-            pltpu.VMEM((quarters,) + attn_weights.shape[1:], low),
-            pltpu.VMEM(cross_weights.shape, low),
-            pltpu.VMEM(self_weights.shape, low),
+            pltpu.VMEM((2, quarters, 3, mem, ffn_chunk.rows, model), low),
+            pltpu.VMEM((2 * quarters, 1, mem, 2, attn_chunk.rows, model), low),
+            pltpu.VMEM((3,) + attn_weights.shape[1:], low),
+            pltpu.VMEM(cross_weights.shape[1:], low),
+            pltpu.VMEM(self_weights.shape[1:], low),
             pltpu.VMEM(sides.shape, low),
             pltpu.VMEM(qkv.shape, low),
             pltpu.VMEM(inputs.shape, low),
             pltpu.VMEM(inputs.shape, low),
-            dma((6,)), dma((1,)), dma((1, mem)), dma((1, mem)),
+            pltpu.VMEM((count * dec_len, model), wide),
+            pltpu.VMEM((count, mem, enc_len // mem, model), low),
+            pltpu.VMEM(output.shape, low),
+            pltpu.VMEM(small_shape, wide),
+            pltpu.VMEM((mem,) + small_shape, wide),
+            pltpu.VMEM((block,) + small_shape, wide),
+            dma((8 + count,)),
+            dma((move_count, mem)), dma((move_count, mem)), dma((move_count,)),
+            dma((mem + block,)), dma((mem + block,)),
         ]
-        + reduction_scratch(Chunk(2, 0, own_hidden), mem, model),
+        + reduction_scratch(ffn_chunk, mem, model)
+        + reduction_scratch(attn_chunk, mem, model),
         compiler_params=pltpu.CompilerParams(
-            collective_id=2, has_side_effects=True, vmem_limit_bytes=63000000
+            collective_id=1, has_side_effects=True, vmem_limit_bytes=66000000
         ),
     )(
         *ffn, attn_weights, cross_weights, self_weights, sides, qkv, output,
         grad_second, first, inputs, normed_one, normed_two, self_mixed, cross_mixed, queries,
-        memory, gains,
+        memory, gains, gain_three,
     )
 
 
@@ -1129,50 +1121,25 @@
     grad_wide = grad_out.astype(wide)
     back, gain_three = rms_back(second, scale_three, gain_values[2], grad_three)
     grad_second = grad_wide + back
-    (
-        ffn_sums, output, grad_qkv, grad_self_out, grad_cross_query, grad_cross_kv,
-        grad_cross_out, grad_memory, grad_input, gain_sums, distance_sums,
-    ) = back_all(
+    attn_sums, ffn_sums, output, grad_memory, grad_input, small = back_all(
         ffn_grads, attn_weights_in, cross_weights, self_weights, cross_sides, qkv,
         jnp.stack(relative(output.astype(low), 1, mem)),
         grad_second, first, own_input, normed_one, normed_two, self_mixed, cross_mixed,
-        cross_queries, memory, gain_values, lane_count,
-    )
-    attn_grads = [
-        grad.reshape(-1, mem, own_width, model)
-        for grad in (grad_qkv, grad_self_out, grad_cross_query, grad_cross_kv, grad_cross_out)
-    ]
-
-    def one_hot_of(ids):
-        return (ids[:, None] == jnp.arange(bucket_count)[None, :]).astype(wide)
-
+        cross_queries, memory, gain_values, gain_three[None], lane_count,
+    )
+    attn_sums = sum_blocks(attn_sums).astype(wide)
+    ffn_sums = sum_blocks(ffn_sums).astype(wide)
+    small = sum_blocks(small[:, 0])
+    heads = mem * own_heads
+    gain_sums = lax.dynamic_slice_in_dim(
+        small[heads:].reshape(3, model), me * own_width, own_width, 1
+    )
     falling = jnp.concatenate(
         [jnp.flip(buckets), jnp.full((lane_count - dec_len,), -1, buckets.dtype)]
     )
-    grad_table = jnp.einsum(
-        "lb,hl->hb",
-        one_hot_of(falling),
-        jnp.sum(distance_sums, axis=0).reshape(2 * pairs, lane_count),
-        precision=highest,
-    )
-    gain_grads = jnp.concatenate(
-        relative(jnp.concatenate([gain_sums, gain_three[None]]), 1, mem), axis=0
-    ).reshape(mem, 3 * own_width)
-    small = jnp.concatenate(
-        [gain_grads, grad_table.reshape(mem, own_heads * bucket_count)], axis=1
-    )
-    small_size = small.shape[1]
-    small = jnp.pad(small, ((0, 0), (0, 8 * pair - small_size))).reshape(mem, 8, pair)
-    attn_sums, grad_memory, grad_input, small = reduce_all(
-        attn_grads,
-        grad_memory.reshape(count, mem, enc_len // mem, model),
-        jnp.stack(relative(grad_input.astype(low), 1, mem)),
-        small,
-    )
-    attn_sums = sum_blocks(attn_sums).astype(wide)
-    ffn_sums = sum_blocks(ffn_sums).astype(wide)
-    small = sum_blocks(small).reshape(-1)
-    split = 3 * own_width
+    one_hot = (falling[:, None] == jnp.arange(bucket_count)[None, :]).astype(wide)
+    own_sums = lax.dynamic_slice_in_dim(small, me * own_heads, own_heads, 0)
+    grad_table = jnp.einsum("hl,lb->bh", own_sums, one_hot, precision=highest)
 
     def columns(values):
         return jnp.swapaxes(values, -1, -2)
@@ -1181,11 +1148,11 @@
         output.reshape(group, -1, model).astype(wide),
         grad_input.reshape(group, -1, model).astype(wide),
         grad_memory.reshape(group, -1, model).astype(wide),
-        small[:split].reshape(3, own_width),
+        gain_sums,
         columns(attn_sums[0]),
         columns(attn_sums[1:3]),
         attn_sums[3],
-        small[split:small_size].reshape(own_heads, bucket_count).T,
+        grad_table,
         columns(attn_sums[4]),
         columns(attn_sums[5:7]),
         attn_sums[7],

time: 367 us -> 334 us (0.910)
  Pallas kernels: 294 us -> 261 us
  matrix products: 23.1 us -> 27.1 us
    pallas_call x2 -> x1, Pallas kernels: 180 us -> 148 us  [back_all(): pl.pallas_call(back_body, in_specs=[in_place] * 7 + [held] * 12, out_spec...]
    unnamed x62 -> x73, local copies, waits for them, and re-layouts: 12.8 us -> 10.2 us
where the time goes in v3:
time: 334 us; the launch traced here: 331 us
  Pallas kernels  261 us (78%)
  matrix products  27.1 us (8%)
  local copies, waits for them, and re-layouts  24.8 us (7%)
  other arithmetic  15.9 us (5%)
    pallas_call x1, Pallas kernels, back_all(): pl.pallas_call(back_body, in_specs=[in_place] * 7 + [held] * 12, out_spec...  148 us
    pallas_call x1, Pallas kernels, gather_all(): pl.pallas_call(gather_body, in_specs=[held, held, in_place] + [held] * (l...  114 us
    dot_general x2, matrix products, weight_grad(): jnp.einsum('rtc,rtd->cd', grads, values, preferred_element_type=wide)  12.7 us
    unnamed x73, local copies, waits for them, and re-layouts  10.2 us
    dot_general x2, matrix products, times_t(): jnp.einsum('rtd,cd->rtc', values, weight, preferred_element_type=wide)  9 us

profile of v3, /device:TPU:25, one launch (start us, length us, event | category | flops | bytes accessed | tf_op | source)
XLA Modules:
  0.0 330.7 jit_solution(1946473300587128419)
XLA Ops:
  0.7 0.9 fusion.27
  2.2 1.2 fusion.9
  3.5 0.7 convert_element_type.64.gain_ref
  4.2 1.0 fusion.11.normed_ref.normed_one_ref
  5.2 0.8 copy.38.dec_column_ref
  6.7 1.5 fusion.26
  8.7 2.9 pad_maximum_fusion.1.ffn_ref
  11.8 0.8 copy-done.14
  13.8 0.7 pad_add_fusion.1
  15.9 113.9 %shard_map.255 = (bf16[8,4,192,768]{3,2,1,0:T(8,128)(2,1)}, bf16[2,4,512,768]{3,2,1,0:T(8,128)(2,1)}, bf16[1,4,512,768]{3,2,1,0:T(8,128)(2,1)}, bf16[2,4,128,768...) custom-call(bf16[8,192,768]{2,1,0:T(8,128)(2,1)} %copy-done.5, ...), custom_call_target="tpu_custom_call" | custom-call | tf_op jit(solution)/shard_map/pallas_call | solution.py:398
  129.8 1.5 slice.77
  131.5 0.7 multiply_reduce_fusion.2
  132.3 5.4 %fusion.15 = f32[2,176,4096]{2,1,0:T(8,128)S(1)} fusion(bf16[4096,768,1]{1,0,2:T(8,128)(2,1)} %bitcast.124, f32[2,176,768]{2,1,0:T(8,128)S(1)} %get-tuple-element.103, f32[768]{0:T(1024)S(1)} %get-tuple-element.79, f32[2,176]{1,0:T(2,128)S(1)} %add_rsqrt_fusion), kind=kOutput, calls=%fused_computation.57 | convolution fusion | flops 2215403520 | bytes 13144448 | tf_op jit(solution)/shard_map/rtd,cd->rtc/dot_general | solution.py:1020
  137.7 3.6 %fusion.6 = (bf16[2,176,2048]{2,1,0:T(8,128)(2,1)S(1)}, bf16[2,176,2048]{2,1,0:T(8,128)(2,1)S(1)}, bf16[2,176,2048]{2,1,0:T(8,128)(2,1)S(1)}) fusion(f32[2,176,4096]{2,1,0:T(8,128)S(1)} %fusion.15, bf16[2048,768,1]{1,0,2:T(8,128)(2,1)S(1)} %bitcast.128, bf16[8,176,768]{2,1,0:T(8,128)(2,1)S(1)} %copy-done.17, s32[]{:T(128)S(6)} %select_n.73), kind=kOutput, calls=%fused_computation.11 | convolution fusion | flops 1126039552 | bytes 13778948 | tf_op jit(solution)/shard_map/rtd,cd->rtc/dot_general | solution.py:1020
  141.4 2.6 multiply_reduce_fusion
  144.0 1.3 subtract_add_fusion.grad_second_ref
  145.9 1.3 fusion.8
  147.4 0.9 pad_maximum_fusion.4.output_ref
  148.3 8.2 %bitcast_convert_fusion = bf16[4096,768]{1,0:T(8,128)(2,1)} fusion(bf16[2,176,2048]{2,1,0:T(8,128)(2,1)} %copy-done.25, bf16[2,176,2048]{2,1,0:T(8,128)(2,1)} %copy-done.24, f32[2,176,768]{2,1,0:T(8,128)S(1)} %get-tuple-element.103, f32[768]{0:T(1024)S(1)} %get-tuple-element.79, f32[2,176]{1,0:T(2,128)S(1)} %add_rsqrt_fusion), kind=kOutput, calls=%fused_computation | convolution fusion | flops 2224316416 | bytes 10260864 | tf_op jit(solution)/shard_map/rtc,rtd->cd/dot_general | solution.py:1028
  156.4 4.6 %bitcast_convert_fusion.1 = bf16[2048,768]{1,0:T(8,128)(2,1)} fusion(bf16[2,176,2048]{2,1,0:T(8,128)(2,1)S(1)} %copy-done.23, bf16[8,176,768]{2,1,0:T(8,128)(2,1)} %param.31, s32[]{:T(128)S(6)} %select_n.73), kind=kOutput, calls=%fused_computation.1 | convolution fusion | flops 1108869120 | bytes 5128196 | tf_op jit(solution)/shard_map/rtc,rtd->cd/dot_general | solution.py:1028
  161.0 147.5 %shard_map.256 = (bf16[8,192,768]{2,1,0:T(8,128)(2,1)}, bf16[3,512,768]{2,1,0:T(8,128)(2,1)}, bf16[4,2,44,768]{3,2,1,0:T(8,128)(2,1)}, bf16[4,2,128,768]{3,2,1,0...) custom-call(bf16[2,4,512,768]{3,2,1,0:T(8,128)(2,1)} %bitcast.115, ...), custom_call_target="tpu_custom_call" | custom-call | tf_op jit(solution)/shard_map/pallas_call | solution.py:878
  308.5 2.1 convert_element_type.82
  310.6 2.1 copy-done.2
  312.9 2.4 copy.41
  315.3 2.1 convert_element_type.81
  317.4 1.4 slice_bitcast_fusion.4
  318.8 1.6 slice_bitcast_fusion.2
  320.4 2.7 slice_bitcast_fusion.1
  323.5 1.6 copy.39
  325.1 1.6 copy.40
  326.7 2.0 bitcast_convert_fusion.2
  329.6 0.8 fusion.16
  (93 shorter events, 6.9 us)
Async XLA Ops:
  0.6 4.6 %copy-start = (s32[8,176]{1,0:T(8,128)S(1)}, s32[8,176]{1,0:T(8,128)}, u32[]{:S(2)}) copy-start(s32[8,176]{1,0:T(8,128)} %param.18) | copy-start | bytes 16900
  3.5 5.0 %copy-start.3 = (bf16[2,176,768]{2,1,0:T(8,128)(2,1)}, bf16[2,176,768]{2,1,0:T(8,128)(2,1)S(1)}, u32[]{:S(2)}) copy-start(bf16[2,176,768]{2,1,0:T(8,128)(2,1)S(1)} %get-tuple-element.82.input_ref) | copy-start | bytes 1622020
  4.2 4.2 %copy-start.16 = (f32[3,768]{1,0:T(4,128)}, f32[3,768]{1,0:T(4,128)S(1)}, u32[]{:S(2)}) copy-start(f32[3,768]{1,0:T(4,128)S(1)} %convert_element_type.64.gain_ref) | copy-start | bytes 27652
  8.7 2.9 copy-start.12
  8.7 3.0 copy-start.10
  8.7 3.0 copy-start.13
  11.6 1.0 copy-start.14
  11.6 1.2 copy-start.11
  11.6 1.2 copy-start.15
  11.6 1.2 copy-start.19
  11.7 3.5 %copy-start.20 = (bf16[32,3]{0,1:T(4,128)(2,1)S(1)}, bf16[32,3]{0,1:T(4,128)(2,1)}, u32[]{:S(2)}) copy-start(bf16[32,3]{0,1:T(4,128)(2,1)} %param.25) | copy-start | bytes 580
  12.9 3.0 copy-start.5
  129.8 1.6 copy-start.4
  129.8 1.7 copy-start.6
  132.2 5.4 %copy-start.17 = (bf16[8,176,768]{2,1,0:T(8,128)(2,1)S(1)}, bf16[8,176,768]{2,1,0:T(8,128)(2,1)}, u32[]{:S(2)}) copy-start(bf16[8,176,768]{2,1,0:T(8,128)(2,1)} %param.31) | copy-start | bytes 6488068
  132.2 5.4 %copy-start.21 = (bf16[1,4,512,768]{3,2,1,0:T(8,128)(2,1)S(1)}, bf16[1,4,512,768]{3,2,1,0:T(8,128)(2,1)}, u32[]{:S(2)}) copy-start(bf16[1,4,512,768]{3,2,1,0:T(8,128)(2,1)} %get-tuple-element.32) | copy-start | bytes 9437188
  132.2 9.1 %slice-start = ((s8[6291456]{0:T(1024)(128)(4,1)}), s8[4194304]{0:T(1024)(128)(4,1)S(1)}, s32[]{:S(2)}) async-start(s8[6291456]{0:T(1024)(128)(4,1)} %bitcast.125), calls=%async_computation | async-start | bytes 8388608
  137.7 3.7 %slice-start.1 = ((s8[6291456]{0:T(1024)(128)(4,1)}), s8[2097152]{0:T(1024)(128)(4,1)S(1)}, s32[]{:S(2)}) async-start(s8[6291456]{0:T(1024)(128)(4,1)} %bitcast.125), calls=%async_computation.1 | async-start | bytes 4194304
  141.3 2.7 copy-start.24
  141.3 2.6 copy-start.25
  141.3 4.5 %copy-start.22 = (bf16[2,176,2048]{2,1,0:T(8,128)(2,1)}, bf16[2,176,2048]{2,1,0:T(8,128)(2,1)S(1)}, u32[]{:S(2)}) copy-start(bf16[2,176,2048]{2,1,0:T(8,128)(2,1)S(1)} %get-tuple-element.85) | copy-start | bytes 4325380
  148.3 8.2 %copy-start.23 = (bf16[2,176,2048]{2,1,0:T(8,128)(2,1)S(1)}, bf16[2,176,2048]{2,1,0:T(8,128)(2,1)}, u32[]{:S(2)}) copy-start(bf16[2,176,2048]{2,1,0:T(8,128)(2,1)} %copy-done.22) | copy-start | bytes 4325380
  310.6 2.1 copy-start.2
  320.4 2.8 copy-start.8
  320.4 2.8 copy-start.9
  323.4 3.2 copy-start.7
  326.7 3.8 %copy-start.1 = (s32[8,176]{1,0:T(8,128)S(1)}, s32[8,176]{1,0:T(8,128)}, u32[]{:S(2)}) copy-start(s32[8,176]{1,0:T(8,128)} %param.18) | copy-start | bytes 16900
  326.7 2.1 copy-start.18
